TPU v7x, 128 devices: a whole 4x4x4 slice. The times are simulated.
128 devices in a mesh: section: 8 (over x, z_hi), tensor: 4 (over z_lo, core), dp: 4 (over y).
Axes of the slice: x: 4, y: 4, z: 4 (z_hi: 2, z_lo: 2; z = z_hi * 2 + z_lo), core: 2. Of those that a mesh axis runs over, the one named last changes fastest.
Arguments:
- tokens: bfloat16 [64, 4096], P(None, ('section', 'dp')), may hold values from -100 to 100
- attn_gain: float32 [4096], P(('section', 'dp')), may hold values from 0.1 to 1.9
- qkv_weight: bfloat16 [4096, 10240], P(('section', 'dp'), 'tensor'), may hold values from -0.09375 to 0.09375
- qkv_order: int32 [10], replicated, may hold values from 0 to 9, each once
- cache_keys: bfloat16 [64, 8, 4096, 128], P(('section', 'dp'), 'tensor'), may hold values from -1300 to 1300
- cache_values: bfloat16 [64, 8, 4096, 128], P(('section', 'dp'), 'tensor'), may hold values from -6 to 6
- cache_len: int32 [64], P(('section', 'dp')), may hold values from 2 to 4096, as said below
- out_weight: bfloat16 [8192, 4096], P('tensor', ('section', 'dp')), may hold values from -0.0625 to 0.0625
- ffn_gain: float32 [4096], P(('section', 'dp')), may hold values from 0.1 to 1.9
- gate_up: bfloat16 [2, 4096, 28672], P(None, ('section', 'dp'), 'tensor'), may hold values from -0.09375 to 0.09375
- down_weight: bfloat16 [28672, 4096], P('tensor', ('section', 'dp')), may hold values from -0.03125 to 0.03125
Outputs:
- layer_out: bfloat16 [64, 4096], P(None, ('section', 'dp'))
Inputs may be any that keep to these rules, and one draw needn't show every extreme that they name: qkv_order is a permutation of 0 to 9, the same for every key-value group. `cache_len`: at least one sequence has all 4096 positions valid.
All inputs are finite; a program needn't handle non-finite values.
Results may differ from a plain program's by a relative error of at most 0.0065.
Values may be sent and summed in bfloat16 or wider, within the bound.
A program may use at most 64 MiB of HBM per device.

v0:
```python
import jax
import jax.numpy as jnp
from jax import lax
from jax.sharding import PartitionSpec as P

D = 4096
HEADS = 64
KV_HEADS = 8
HD = 128
LEN = 4096
GROUP = 10


def copy_for_each(x, axis):
    copies = jnp.broadcast_to(x, (lax.axis_size(axis), *x.shape))
    return lax.all_to_all(copies, axis, split_axis=0, concat_axis=0, tiled=True)


def over_copies(x, axis):
    return copy_for_each(x, axis).sum(axis=0)


def laid_out(pieces, dim):
    pieces = jnp.moveaxis(pieces, 0, dim)
    lengths = pieces.shape
    return pieces.reshape(*lengths[:dim], lengths[dim] * lengths[dim + 1], *lengths[dim + 2 :])


def gather_directly(x, axis, dim):
    pieces = copy_for_each(x, axis)
    return laid_out(pieces, dim)


def split_up(x, dim, count):
    lengths = x.shape
    pieces = x.reshape(*lengths[:dim], count, lengths[dim] // count, *lengths[dim + 1 :])
    return jnp.moveaxis(pieces, dim, 0)


def sent_and_summed(x, axis, dim):
    pieces = split_up(x, dim, lax.axis_size(axis))
    arrived = lax.all_to_all(pieces, axis, split_axis=0, concat_axis=0, tiled=True)
    return arrived.astype(jnp.float32).sum(axis=0)


def normalize(stream, gain_vec):
    wide = stream.astype(jnp.float32)
    squares = over_copies(jnp.sum(wide * wide, axis=1), ("section", "dp"))
    factor = lax.rsqrt(squares / D + 1e-05)
    return (wide * factor[:, None] * gain_vec[None, :]).astype(jnp.bfloat16)


def rotate(vector, cosine, sine_part):
    half_dim = vector.shape[-1] // 2
    first_half = vector[..., :half_dim]
    second = vector[..., half_dim:]
    return jnp.concatenate(
        [first_half * cosine - second * sine_part, second * cosine + first_half * sine_part],
        axis=-1,
    )


def project_rows(row_block, weight_cols):
    return jnp.dot(
        gather_directly(row_block, ("section", "dp"), 0),
        weight_cols,
        preferred_element_type=jnp.float32,
    )


def add_residual(base_rows, partial_sum):
    summed = over_copies(partial_sum, "tensor")
    return (base_rows.astype(jnp.float32) + summed).astype(jnp.bfloat16)


def body(
    tokens,
    attn_gain,
    qkv_weight,
    qkv_order,
    cache_keys,
    cache_values,
    cache_len,
    out_weight,
    ffn_gain,
    gate_up,
    down_weight,
):
    seq_count = cache_len.shape[0]
    local_groups = cache_keys.shape[1]
    per_group = HEADS // KV_HEADS
    normed = normalize(tokens, attn_gain)
    row_block = normed
    joined_cols = sent_and_summed(
        jnp.dot(row_block, qkv_weight, preferred_element_type=jnp.float32).astype(jnp.bfloat16),
        ("section", "dp"),
        0,
    )
    blocks = joined_cols.reshape(seq_count, local_groups, GROUP, HD)
    onehot = (qkv_order[:, None] == jnp.arange(GROUP, dtype=jnp.int32)[None, :]).astype(jnp.float32)
    logical = jnp.einsum("bgjd,ji->bgid", blocks, onehot, precision=lax.Precision.HIGHEST)
    half_dim = HD // 2
    inv_freq = 500000.0 ** (-(2.0 * jnp.arange(half_dim, dtype=jnp.float32)) / HD)
    angles = cache_len.astype(jnp.float32)[:, None] * inv_freq[None, :]
    cosine = jnp.cos(angles)
    sine_part = jnp.sin(angles)
    queries = rotate(
        logical[:, :, :per_group], cosine[:, None, None, :], sine_part[:, None, None, :]
    ).astype(jnp.bfloat16)
    new_key = rotate(logical[:, :, per_group], cosine[:, None, :], sine_part[:, None, :]).astype(
        jnp.bfloat16
    )
    new_value = logical[:, :, per_group + 1].astype(jnp.bfloat16)
    inv_scale = 1.0 / jnp.sqrt(jnp.float32(HD))
    scores = (
        jnp.einsum("bgpd,bgld->bgpl", queries, cache_keys, preferred_element_type=jnp.float32)
        * inv_scale
    )
    own_score = (
        jnp.einsum("bgpd,bgd->bgp", queries, new_key, preferred_element_type=jnp.float32)
        * inv_scale
    )
    valid_mask = jnp.arange(LEN, dtype=jnp.int32)[None, :] < cache_len[:, None]
    masked = jnp.where(valid_mask[:, None, None, :], scores, -jnp.inf)
    peak = jnp.maximum(jnp.max(masked, axis=-1), own_score)
    weights = jnp.exp(masked - peak[..., None])
    own_weight = jnp.exp(own_score - peak)
    denom_sum = jnp.sum(weights, axis=-1) + own_weight
    probabilities = (weights / denom_sum[..., None]).astype(jnp.bfloat16)
    own_prob = (own_weight / denom_sum).astype(jnp.bfloat16)
    mixed_heads = jnp.einsum(
        "bgpl,bgld->bgpd", probabilities, cache_values, preferred_element_type=jnp.float32
    )
    mixed_heads = (
        mixed_heads
        + own_prob.astype(jnp.float32)[..., None] * new_value.astype(jnp.float32)[:, :, None, :]
    )
    attended = mixed_heads.astype(jnp.bfloat16).reshape(seq_count, -1)
    hidden_state = add_residual(tokens, project_rows(attended, out_weight))
    ffn_normed = normalize(hidden_state, ffn_gain)
    row_block = ffn_normed
    gate_and_up = sent_and_summed(
        jnp.einsum("rd,kdf->rkf", row_block, gate_up, preferred_element_type=jnp.float32).astype(
            jnp.bfloat16
        ),
        ("section", "dp"),
        0,
    )
    activated = (jax.nn.silu(gate_and_up[:, 0]) * gate_and_up[:, 1]).astype(jnp.bfloat16)
    return add_residual(hidden_state, project_rows(activated, down_weight))


def solution(mesh):
    return jax.shard_map(
        body,
        mesh=mesh,
        in_specs=(
            P(None, ("section", "dp")),
            P(("section", "dp")),
            P(("section", "dp"), "tensor"),
            P(),
            P(("section", "dp"), "tensor", None, None),
            P(("section", "dp"), "tensor", None, None),
            P(("section", "dp")),
            P("tensor", ("section", "dp")),
            P(("section", "dp")),
            P(None, ("section", "dp"), "tensor"),
            P("tensor", ("section", "dp")),
        ),
        out_specs=P(None, ("section", "dp")),
        check_vma=False,
    )
```

profile of v0, /device:TPU:1, one launch (start us, length us, event | category | flops | bytes accessed | tf_op | source)
XLA Modules:
  0.0 153.6 jit_solution(722798849827678927)
XLA Ops:
  0.0 1.0 fusion.8
  1.0 0.6 broadcast_in_dim.25
  1.6 11.2 %all-to-all-start = ((f32[32,1,64]{2,1,0:T(1,128)}), f32[32,1,64]{2,1,0:T(1,128)S(1)}, u32[]{:S(2)}, u32[]{:S(2)}) async-start(f32[32,1,64]{2,1,0:T(1,128)} %broadcast_in_dim.25), calls=%async_computation | async-start | bytes 32768 | tf_op jit(solution)/shard_map/all_to_all | solution.py:16
  12.8 0.7 iota_compare_fusion
  13.5 0.7 convert_element_type.61
  14.2 7.2 %all-to-all-done = f32[32,1,64]{2,1,0:T(1,128)S(1)} async-done(((f32[32,1,64]{2,1,0:T(1,128)}), f32[32,1,64]{2,1,0:T(1,128)S(1)}, u32[]{:S(2)}, u32[]{:S(2)}) %all-to-all-start) | async-done | bytes 8224 | tf_op jit(solution)/shard_map/all_to_all | solution.py:16
  21.4 1.4 convolution_convert_fusion.1
  22.8 0.8 reshape.154
  23.7 3.9 %all-to-all-start.1 = ((bf16[32,2,2560]{2,1,0:T(2,128)(2,1)}), bf16[32,2,2560]{2,1,0:T(2,128)(2,1)S(1)}, u32[]{:S(2)}, u32[]{:S(2)}) async-start(bf16[32,2,2560]{2,1,0:T(2,128)(2,1)} %reshape.154), calls=%async_computation.1 | async-start | bytes 655360 | tf_op jit(solution)/shard_map/all_to_all | solution.py:42
  27.7 9.8 %all-to-all-done.1 = bf16[32,2,2560]{2,1,0:T(2,128)(2,1)S(1)} async-done(((bf16[32,2,2560]{2,1,0:T(2,128)(2,1)}), bf16[32,2,2560]{2,1,0:T(2,128)(2,1)S(1)}, u32[]{:S(2)}, u32[]{:S(2)}) %all-to-all-start.1) | async-done | bytes 327712 | tf_op jit(solution)/shard_map/all_to_all | solution.py:42
  37.5 0.3 convert_reduce_fusion.1
  37.8 0.9 convolution_bitcast_fusion
  39.0 0.2 fusion.27
  39.2 3.5 %fusion.35 = (f32[2,2,8]{2,1,0:T(2,128)S(1)}, f32[2,2,8,4096]{3,2,1,0:T(8,128)S(1)}) fusion(bf16[2,2,4096,128]{3,2,1,0:T(8,128)(2,1)} %param.15, bf16[2,2,8,64]{3,2,1,0:T(8,128)(2,1)S(1)} %get-tuple-element.10, bf16[2,2,8,64]{3,2,1,0:T(8,128)(2,1)S(1)} %get-tuple-element.9, pred[2,4096]{1,0:T(4,128)(4,1)S(1)} %iota_compare_fusion), kind=kOutput, calls=%fused_computation.67 | convolution fusion | flops 33964000 | bytes 4735104 | tf_op jit(solution)/shard_map/bgpd,bgld->bgpl/dot_general | solution.py:116
  42.7 0.2 fusion.3
  43.0 0.7 fusion.2
  43.8 0.1 broadcast_in_dim.27
  43.9 13.1 %all_to_all.42 = bf16[32,2,2048]{2,1,0:T(2,128)(2,1)S(1)} all-to-all(bf16[32,2,2048]{2,1,0:T(2,128)(2,1)S(1)} %broadcast_in_dim.27), channel_id=1, replica_groups=mesh['section'=8,'tensor'=4,'dp'=4] {'section','dp'}, dimensions={0} | all-to-all | bytes 524288 | tf_op jit(solution)/shard_map/all_to_all | solution.py:16
  57.2 0.2 fusion.36
  57.4 10.3 %all_to_all.43 = f32[4,64,128]{2,1,0:T(8,128)S(1)} all-to-all(f32[4,64,128]{2,1,0:T(8,128)S(1)} %broadcast_in_dim.28), channel_id=1, replica_groups=mesh['section'=8,'tensor'=4,'dp'=4] {'tensor'}, dimensions={0} | all-to-all | bytes 262144 | tf_op jit(solution)/shard_map/all_to_all | solution.py:16
  67.8 12.2 %all_to_all.44 = f32[32,1,64]{2,1,0:T(1,128)S(1)} all-to-all(f32[32,1,64]{2,1,0:T(1,128)S(1)} %broadcast_in_dim.29), channel_id=1, replica_groups=mesh['section'=8,'tensor'=4,'dp'=4] {'section','dp'}, dimensions={0} | all-to-all | bytes 16384 | tf_op jit(solution)/shard_map/all_to_all | solution.py:16
  80.1 4.0 %convolution_convert_fusion = bf16[64,2,7168]{2,0,1:T(8,128)(2,1)} fusion(bf16[2,128,7168]{2,1,0:T(8,128)(2,1)} %param.20, bf16[64,128]{1,0:T(8,128)(2,1)S(1)} %get-tuple-element.6, f32[128]{0:T(128)S(1)} %copy-done.4, f32[64]{0:T(128)S(1)} %add_rsqrt_fusion), kind=kOutput, calls=%fused_computation | convolution fusion | flops 235831296 | bytes 5522176 | tf_op jit(solution)/shard_map/rd,kdf->rkf/dot_general | solution.py:143
  84.1 4.7 %reshape.158 = bf16[32,2,2,7168]{3,1,0,2:T(2,128)(2,1)} reshape(bf16[64,2,7168]{2,0,1:T(8,128)(2,1)} %convolution_convert_fusion) | data formatting | bytes 3670016 | tf_op jit(solution)/shard_map/reshape | solution.py:36
  88.9 2.8 %copy.24 = bf16[32,2,2,7168]{3,1,2,0:T(2,128)(2,1)S(1)} copy(bf16[32,2,2,7168]{3,1,0,2:T(2,128)(2,1)} %reshape.158) | data formatting | bytes 3670016 | tf_op jit(solution)/shard_map/reshape | solution.py:36
  91.6 26.2 %all_to_all.45 = bf16[32,2,2,7168]{3,1,2,0:T(2,128)(2,1)S(1)} all-to-all(bf16[32,2,2,7168]{3,1,2,0:T(2,128)(2,1)S(1)} %copy.24), channel_id=1, replica_groups=mesh['section'=8,'tensor'=4,'dp'=4] {'section','dp'}, dimensions={0} | all-to-all | bytes 3670016 | tf_op jit(solution)/shard_map/all_to_all | solution.py:42
  117.8 1.0 convert_reduce_fusion
  119.0 0.5 broadcast_in_dim.30
  119.5 21.4 %all_to_all.46 = bf16[32,2,7168]{2,1,0:T(2,128)(2,1)S(1)} all-to-all(bf16[32,2,7168]{2,1,0:T(2,128)(2,1)S(1)} %broadcast_in_dim.30), channel_id=1, replica_groups=mesh['section'=8,'tensor'=4,'dp'=4] {'section','dp'}, dimensions={0} | all-to-all | bytes 1835008 | tf_op jit(solution)/shard_map/all_to_all | solution.py:16
  140.9 1.3 reshape.159
  142.2 1.6 %fusion.37 = f32[64,128]{1,0:T(8,128)S(1)} fusion(bf16[64,7168]{1,0:T(8,128)(2,1)} %reshape.159, bf16[7168,128]{1,0:T(8,128)(2,1)S(1)} %copy-done), kind=kOutput, calls=%fused_computation.69 | convolution fusion | flops 117440512 | bytes 2785280 | tf_op jit(solution)/shard_map/dot_general | solution.py:64
  143.8 9.1 %all_to_all.47 = f32[4,64,128]{2,1,0:T(8,128)S(1)} all-to-all(f32[4,64,128]{2,1,0:T(8,128)S(1)} %broadcast_in_dim.31), channel_id=1, replica_groups=mesh['section'=8,'tensor'=4,'dp'=4] {'tensor'}, dimensions={0} | all-to-all | bytes 262144 | tf_op jit(solution)/shard_map/all_to_all | solution.py:16
  152.9 0.6 fusion.15
  (34 shorter events, 0.9 us)
Async XLA Ops:
  0.0 142.2 %copy-start = (bf16[7168,128]{1,0:T(8,128)(2,1)S(1)}, bf16[7168,128]{1,0:T(8,128)(2,1)}, u32[]{:S(2)}) copy-start(bf16[7168,128]{1,0:T(8,128)(2,1)} %param.21) | copy-start | bytes 5505028
  1.6 19.8 %all-to-all-start = ((f32[32,1,64]{2,1,0:T(1,128)}), f32[32,1,64]{2,1,0:T(1,128)S(1)}, u32[]{:S(2)}, u32[]{:S(2)}) async-start(f32[32,1,64]{2,1,0:T(1,128)} %broadcast_in_dim.25), calls=%async_computation | async-start | bytes 32768 | tf_op jit(solution)/shard_map/all_to_all | solution.py:16
  23.7 13.9 %all-to-all-start.1 = ((bf16[32,2,2560]{2,1,0:T(2,128)(2,1)}), bf16[32,2,2560]{2,1,0:T(2,128)(2,1)S(1)}, u32[]{:S(2)}, u32[]{:S(2)}) async-start(bf16[32,2,2560]{2,1,0:T(2,128)(2,1)} %reshape.154), calls=%async_computation.1 | async-start | bytes 655360 | tf_op jit(solution)/shard_map/all_to_all | solution.py:42
  37.8 5.2 %copy-start.1 = (bf16[2,2,4096,128]{3,2,1,0:T(8,128)(2,1)S(1)}, bf16[2,2,4096,128]{3,2,1,0:T(8,128)(2,1)}, u32[]{:S(2)}) copy-start(bf16[2,2,4096,128]{3,2,1,0:T(8,128)(2,1)} %param.16) | copy-start | bytes 12582916
  42.7 14.4 %copy-start.2 = (bf16[2048,128]{1,0:T(8,128)(2,1)S(1)}, bf16[2048,128]{1,0:T(8,128)(2,1)}, u32[]{:S(2)}) copy-start(bf16[2048,128]{1,0:T(8,128)(2,1)} %param.18) | copy-start | bytes 1572868
  43.0 24.7 %copy-start.3 = (bf16[64,128]{1,0:T(8,128)(2,1)S(1)}, bf16[64,128]{1,0:T(8,128)(2,1)}, u32[]{:S(2)}) copy-start(bf16[64,128]{1,0:T(8,128)(2,1)} %param.11) | copy-start | bytes 49156
  43.0 37.1 %copy-start.4 = (f32[128]{0:T(128)S(1)}, f32[128]{0:T(128)}, u32[]{:S(2)}) copy-start(f32[128]{0:T(128)} %param.19) | copy-start | bytes 1540
where the time goes:
time: 154 us
  blocking collectives  92.3 us (60%)
  waiting for transfers between devices  17 us (11%)
  starting transfers between devices  15 us (10%)
  matrix products  12.6 us (8%)
  local copies, waits for them, and re-layouts  11.1 us (7%)
  other arithmetic  5.15 us (3%)
    all_to_all x5, blocking collectives, copy_for_each(): return lax.all_to_all(copies, axis, split_axis=0, concat_axis=0, tiled=True)  66.1 us
    all_to_all x1, blocking collectives, sent_and_summed(): lax.all_to_all(pieces, axis, split_axis=0, concat_axis=0, tiled=True)  26.2 us
    all_to_all x1, starting transfers between devices, copy_for_each(): return lax.all_to_all(copies, axis, split_axis=0, concat_axis=0, tiled=True)  11.2 us
    all_to_all x1, waiting for transfers between devices, sent_and_summed(): lax.all_to_all(pieces, axis, split_axis=0, concat_axis=0, tiled=True)  9.85 us
    reshape x3, local copies, waits for them, and re-layouts, split_up(): x.reshape(*lengths[:dim], count, lengths[dim] // count, *lengths[dim + 1:])  8.34 us
    all_to_all x1, waiting for transfers between devices, copy_for_each(): return lax.all_to_all(copies, axis, split_axis=0, concat_axis=0, tiled=True)  7.19 us
    dot_general x1, matrix products, body(): jnp.einsum('rd,kdf->rkf', row_block, gate_up, preferred_element_type=jnp....  3.99 us
    all_to_all x1, starting transfers between devices, sent_and_summed(): lax.all_to_all(pieces, axis, split_axis=0, concat_axis=0, tiled=True)  3.88 us
  transfers between devices with their start and end apart: 2, of which 2 were waited for; matrix products, arithmetic and copies ran while one was open for 1% of the time, Pallas kernels for 0%

commit v1 on v0

v1 whole, which is shorter than its diff:
```python
import jax
import jax.numpy as jnp
from jax import lax
from jax.experimental import pallas as pl
from jax.experimental.pallas import tpu as pltpu
from jax.sharding import PartitionSpec as P

D = 4096
HEADS = 64
KV_HEADS = 8
HD = 128
FF = 28672
LEN = 4096
GROUP = 10
B = 64
RANKS = 32
TENSOR = 4
DP = 4
SEQS = B // RANKS
LOCAL_GROUPS = KV_HEADS // TENSOR
PER_GROUP = HEADS // KV_HEADS
COLS = D // RANKS
SLOT_ROWS = 24
LOCAL_HEADS = HEADS // TENSOR
UNITS = FF // TENSOR
ROW_BLOCKS = 4
COL_BLOCKS = RANKS // ROW_BLOCKS
ROWS_EACH = B // ROW_BLOCKS
UNITS_EACH = UNITS // COL_BLOCKS
MESH = pl.DeviceIdType.MESH
F32 = jnp.float32
BF16 = jnp.bfloat16


def layer_kernel(
    order_ref,
    len_ref,
    tables_hbm,
    tokens_hbm,
    gains_hbm,
    qkv_hbm,
    keys_hbm,
    values_hbm,
    outw_hbm,
    gate_up_hbm,
    down_hbm,
    out_ref,
    tables,
    tokens,
    gains,
    qkvw,
    keys,
    values,
    outw,
    gate_up,
    down,
    joined32,
    joined_out,
    joined_in,
    att_out,
    att_in,
    att32,
    proj1,
    proj2,
    sq_out,
    sq_in,
    gu_out,
    gu_in,
    act,
    load_sem,
    send_sem,
    recv_sem,
):
    section = lax.axis_index("section")
    dp = lax.axis_index("dp")
    tensor = lax.axis_index("tensor")
    rank = section * DP + dp

    def load(i, src, dst):
        return pltpu.make_async_copy(src, dst, load_sem.at[i])

    loads = [
        load(0, tokens_hbm, tokens),
        load(1, gains_hbm, gains),
        load(2, qkv_hbm, qkvw),
        load(3, tables_hbm, tables),
        load(4, keys_hbm, keys),
        load(5, values_hbm, values),
        load(6, outw_hbm, outw),
        load(7, gate_up_hbm, gate_up),
        load(8, down_hbm, down),
    ]
    for copy in loads:
        copy.start()

    def peer(k):
        other = lax.rem(rank + k, RANKS)
        return other, {"section": other // DP, "dp": lax.rem(other, DP)}

    def tensor_peer(k):
        return {"tensor": lax.rem(tensor + k, TENSOR)}

    barrier = pltpu.get_barrier_semaphore()

    def greet(k, carry):
        pl.semaphore_signal(barrier, inc=1, device_id=peer(k)[1], device_id_type=MESH)
        return carry

    lax.fori_loop(1, RANKS, greet, 0)
    for k in range(1, TENSOR):
        pl.semaphore_signal(barrier, inc=1, device_id=tensor_peer(k), device_id_type=MESH)

    loads[0].wait()
    loads[1].wait()
    wide = tokens[...].astype(F32)
    squares = jnp.sum(wide * wide, axis=1, keepdims=True)
    left = jnp.broadcast_to(squares, (B, HD))
    for i in range(3):
        part = left.astype(BF16).astype(F32)
        joined32[:, 20 + i, :] = part
        left = left - part
    joined32[:, 23, :] = jnp.zeros((B, HD), F32)
    scaled = (wide * gains[0:1, :]).astype(BF16)
    loads[2].wait()
    for j in range(LOCAL_GROUPS * GROUP // 2):
        product = jnp.dot(scaled, qkvw[:, j * 256 : j * 256 + 256], preferred_element_type=F32)
        joined32[:, 2 * j, :] = product[:, :HD]
        joined32[:, 2 * j + 1, :] = product[:, HD:]

    def pack(i, carry):
        rows = joined32[pl.ds(i * SEQS, SEQS)]
        joined_out[i] = rows.reshape(SEQS * SLOT_ROWS, HD).astype(BF16)
        return carry

    lax.fori_loop(0, RANKS, pack, 0)
    joined_in[rank] = joined_out[rank]

    pl.semaphore_wait(barrier, RANKS - 1 + TENSOR - 1)

    def remote(src, dst, i, device):
        return pltpu.make_async_remote_copy(
            src_ref=src,
            dst_ref=dst,
            send_sem=send_sem.at[i],
            recv_sem=recv_sem.at[i],
            device_id=device,
            device_id_type=MESH,
        )

    def send_joined(k, carry):
        other, device = peer(k)
        remote(joined_out.at[other], joined_in.at[rank], 0, device).start()
        return carry

    lax.fori_loop(1, RANKS, send_joined, 0)

    def wait_all(src, dst, i):
        whole = remote(src, dst, i, peer(1)[1])
        whole.wait_send()
        whole.wait_recv()

    rest = pl.ds(0, RANKS - 1)
    wait_all(joined_out.at[rest], joined_in.at[rest], 0)

    joined = joined_in[0].astype(F32)
    for i in range(1, RANKS):
        joined = joined + joined_in[i].astype(F32)

    loads[3].wait()
    loads[4].wait()
    loads[5].wait()
    inv_scale = HD**-0.5
    position = lax.broadcasted_iota(jnp.int32, (PER_GROUP, LEN), 1)
    logical_row = lax.broadcasted_iota(jnp.int32, (16, HD), 0)
    for b in range(SEQS):
        base = b * SLOT_ROWS
        total = joined[base + 20 : base + 21] + joined[base + 21 : base + 22] + joined[base + 22 : base + 23]
        factor = lax.rsqrt(total / D + 1e-05)
        for g in range(LOCAL_GROUPS):
            logical = jnp.zeros((16, HD), F32)
            for j in range(GROUP):
                row = joined[base + g * GROUP + j : base + g * GROUP + j + 1]
                logical = jnp.where(logical_row == order_ref[j], row, logical)
            logical = logical * factor
            rotated = logical * tables[b : b + 1] + pltpu.roll(logical, HD // 2, 1) * tables[SEQS + b : SEQS + b + 1]
            rotated = rotated.astype(BF16)
            queries = rotated[0:PER_GROUP]
            new_key = rotated.astype(F32)[PER_GROUP : PER_GROUP + 1]
            new_value = logical[PER_GROUP + 1 : PER_GROUP + 2].astype(BF16).astype(F32)
            own = jnp.sum(queries.astype(F32) * new_key, axis=1, keepdims=True)
            scores = lax.dot_general(
                queries, keys[b, g], (((1,), (1,)), ((), ())), preferred_element_type=F32
            )
            masked = jnp.where(position < len_ref[b], scores, -jnp.inf)
            peak = jnp.maximum(jnp.max(masked, axis=1, keepdims=True), own)
            weights = jnp.exp((masked - peak) * inv_scale)
            own_weight = jnp.exp((own - peak) * inv_scale)
            denom = jnp.sum(weights, axis=1, keepdims=True) + own_weight
            mixed = jnp.dot(weights.astype(BF16), values[b, g], preferred_element_type=F32)
            mixed = mixed + own_weight.astype(BF16).astype(F32) * new_value
            att_out[pl.ds((b * LOCAL_GROUPS + g) * PER_GROUP, PER_GROUP)] = mixed / denom

    att_in[rank] = att_out[...].astype(BF16)

    def send_attended(k, carry):
        other, device = peer(k)
        remote(att_in.at[rank], att_in.at[rank], 1, device).start()
        return carry

    lax.fori_loop(1, RANKS, send_attended, 0)
    wait_all(att_in.at[rest], att_in.at[rest], 1)

    def widen(i, carry):
        att32[pl.ds(i * SEQS, SEQS)] = att_in[i].astype(F32).reshape(SEQS, LOCAL_HEADS, HD)
        return carry

    lax.fori_loop(0, RANKS, widen, 0)
    loads[6].wait()
    attended = jnp.concatenate([att32[:, h, :].astype(BF16) for h in range(LOCAL_HEADS)], axis=1)
    partial = jnp.dot(attended, outw[...], preferred_element_type=F32)

    def sum_over_tensor(value, buffer, i):
        buffer[tensor] = value
        for k in range(1, TENSOR):
            remote(buffer.at[tensor], buffer.at[tensor], i, tensor_peer(k)).start()
        others = pl.ds(0, TENSOR - 1)
        whole = remote(buffer.at[others], buffer.at[others], i, tensor_peer(1))
        whole.wait_send()
        whole.wait_recv()
        return buffer[0] + buffer[1] + buffer[2] + buffer[3]

    projected = sum_over_tensor(partial, proj1, 2)
    hidden = (tokens[...].astype(F32) + projected).astype(BF16).astype(F32)

    squares = jnp.sum(hidden * hidden, axis=1, keepdims=True)
    row_of = lax.broadcasted_iota(jnp.int32, (B, HD), 0)
    lane_of = lax.broadcasted_iota(jnp.int32, (B, HD), 1)
    sq_out[...] = jnp.sum(jnp.where(row_of == lane_of, squares, 0.0), axis=0, keepdims=True)
    sq_in[rank] = sq_out[...]

    def send_squares(k, carry):
        other, device = peer(k)
        remote(sq_out, sq_in.at[rank], 3, device).start()
        return carry

    lax.fori_loop(1, RANKS, send_squares, 0)
    scaled = (hidden * gains[1:2, :]).astype(BF16)
    loads[7].wait()
    my_rows = rank // COL_BLOCKS
    my_units = lax.rem(rank, COL_BLOCKS)

    def block_of(a, c):
        rows = pl.ds(pl.multiple_of(a * ROWS_EACH, ROWS_EACH), ROWS_EACH)
        units = pl.ds(pl.multiple_of(c * UNITS_EACH, 128), UNITS_EACH)
        return rows, units

    def produce(i, carry):
        c = lax.rem(my_units + i, COL_BLOCKS)
        units = pl.ds(pl.multiple_of(c * UNITS_EACH, 128), UNITS_EACH)
        for half in range(2):
            product = jnp.dot(scaled, gate_up[half, :, units], preferred_element_type=F32)
            gu_out[half, :, units] = product.astype(BF16)

        def send_block(j, inner):
            a = lax.rem(my_rows + j, ROW_BLOCKS)
            other = a * COL_BLOCKS + c
            rows, _ = block_of(a, c)

            @pl.when(other != rank)
            def _():
                device = {"section": other // DP, "dp": lax.rem(other, DP)}
                remote(gu_out.at[:, rows, units], gu_in.at[rank], 4, device).start()

            return inner

        lax.fori_loop(0, ROW_BLOCKS, send_block, 0)
        return carry

    lax.fori_loop(0, COL_BLOCKS, produce, 0)
    rows, units = block_of(my_rows, my_units)
    gu_in[rank] = gu_out[:, rows, units]
    wait_all(sq_in.at[rest], sq_in.at[rest], 3)
    total = jnp.sum(sq_in[...], axis=0)
    mine = lax.broadcasted_iota(jnp.int32, (ROWS_EACH, HD), 0) + my_rows * ROWS_EACH
    lane_of = lax.broadcasted_iota(jnp.int32, (ROWS_EACH, HD), 1)
    total = jnp.sum(jnp.where(mine == lane_of, total, 0.0), axis=1, keepdims=True)
    factor = lax.rsqrt(total / D + 1e-05)
    wait_all(gu_in.at[rest], gu_in.at[rest], 4)
    for j in range(UNITS_EACH // 128):
        lanes = slice(j * 128, j * 128 + 128)

        def add(i, sums):
            return (
                sums[0] + gu_in[i, 0, :, lanes].astype(F32),
                sums[1] + gu_in[i, 1, :, lanes].astype(F32),
            )

        zero = jnp.zeros((ROWS_EACH, 128), F32)
        gate, up = lax.fori_loop(0, RANKS, add, (zero, zero), unroll=8)
        gate = gate * factor
        up = up * factor
        value = gate / (1.0 + jnp.exp(-gate)) * up
        act[rows, pl.ds(pl.multiple_of(my_units * UNITS_EACH + j * 128, 128), 128)] = value.astype(BF16)

    def send_activated(k, carry):
        other, device = peer(k)
        remote(act.at[rows, units], act.at[rows, units], 5, device).start()
        return carry

    lax.fori_loop(1, RANKS, send_activated, 0)
    whole = remote(gu_in.at[rest, 0], gu_in.at[rest, 0], 5, peer(1)[1])
    whole.wait_send()
    whole.wait_recv()
    loads[8].wait()
    partial = jnp.dot(act[...], down[...], preferred_element_type=F32)
    lowered = sum_over_tensor(partial, proj2, 6)
    out_ref[...] = (hidden + lowered).astype(BF16)


def body(
    tokens,
    attn_gain,
    qkv_weight,
    qkv_order,
    cache_keys,
    cache_values,
    cache_len,
    out_weight,
    ffn_gain,
    gate_up,
    down_weight,
):
    half_dim = HD // 2
    inv_freq = 500000.0 ** (-(2.0 * jnp.arange(half_dim, dtype=F32)) / HD)
    angles = cache_len.astype(F32)[:, None] * inv_freq[None, :]
    cosine = jnp.cos(angles)
    sine = jnp.sin(angles)
    tables = jnp.concatenate(
        [jnp.concatenate([cosine, cosine], axis=1), jnp.concatenate([-sine, sine], axis=1)], axis=0
    )
    gains = jnp.stack([attn_gain, ffn_gain])
    smem = pl.BlockSpec(memory_space=pltpu.SMEM)
    hbm = pl.BlockSpec(memory_space=pl.ANY)
    return pl.pallas_call(
        layer_kernel,
        out_shape=jax.ShapeDtypeStruct((B, COLS), BF16),
        in_specs=[smem, smem] + [hbm] * 9,
        out_specs=pl.BlockSpec(memory_space=pltpu.VMEM),
        scratch_shapes=[
            pltpu.VMEM((2 * SEQS, HD), F32),
            pltpu.VMEM((B, COLS), BF16),
            pltpu.VMEM((2, COLS), F32),
            pltpu.VMEM(qkv_weight.shape, BF16),
            pltpu.VMEM(cache_keys.shape, BF16),
            pltpu.VMEM(cache_values.shape, BF16),
            pltpu.VMEM(out_weight.shape, BF16),
            pltpu.VMEM(gate_up.shape, BF16),
            pltpu.VMEM(down_weight.shape, BF16),
            pltpu.VMEM((B, SLOT_ROWS, HD), F32),
            pltpu.VMEM((RANKS, SEQS * SLOT_ROWS, HD), BF16),
            pltpu.VMEM((RANKS, SEQS * SLOT_ROWS, HD), BF16),
            pltpu.VMEM((SEQS * LOCAL_HEADS, HD), F32),
            pltpu.VMEM((RANKS, SEQS * LOCAL_HEADS, HD), BF16),
            pltpu.VMEM((B, LOCAL_HEADS, HD), F32),
            pltpu.VMEM((TENSOR, B, COLS), F32),
            pltpu.VMEM((TENSOR, B, COLS), F32),
            pltpu.VMEM((1, 128), F32),
            pltpu.VMEM((RANKS, 1, 128), F32),
            pltpu.VMEM((2, B, UNITS), BF16),
            pltpu.VMEM((RANKS, 2, ROWS_EACH, UNITS_EACH), BF16),
            pltpu.VMEM((B, UNITS), BF16),
            pltpu.SemaphoreType.DMA((9,)),
            pltpu.SemaphoreType.DMA((7,)),
            pltpu.SemaphoreType.DMA((7,)),
        ],
        compiler_params=pltpu.CompilerParams(
            collective_id=0, has_side_effects=True, vmem_limit_bytes=60 * 2**20
        ),
        name="decoder_layer",
    )(
        qkv_order,
        cache_len,
        tables,
        tokens,
        gains,
        qkv_weight,
        cache_keys,
        cache_values,
        out_weight,
        gate_up,
        down_weight,
    )


def solution(mesh):
    rows = P(None, ("section", "dp"))
    return jax.shard_map(
        body,
        mesh=mesh,
        in_specs=(
            rows,
            P(("section", "dp")),
            P(("section", "dp"), "tensor"),
            P(),
            P(("section", "dp"), "tensor", None, None),
            P(("section", "dp"), "tensor", None, None),
            P(("section", "dp")),
            P("tensor", ("section", "dp")),
            P(("section", "dp")),
            P(None, ("section", "dp"), "tensor"),
            P("tensor", ("section", "dp")),
        ),
        out_specs=rows,
        check_vma=False,
    )
```

time: 154 us -> 86.5 us (0.56)
  blocking collectives: 92.3 us -> 0 us
  Pallas kernels: 0 us -> 82.1 us
  waiting for transfers between devices: 17 us -> 0 us
  starting transfers between devices: 15 us -> 0 us
  matrix products: 12.6 us -> 0 us
  local copies, waits for them, and re-layouts: 11.1 us -> 1.32 us
  other arithmetic: 5.15 us -> 2.68 us
    all_to_all x6 -> x0, blocking collectives: 92.3 us -> none  [the longest x5 66.1 us: copy_for_each(): return lax.all_to_all(copies, axis, split_axis=0, concat_axis=0, tiled=True)]
    pallas_call x0 -> x1, Pallas kernels: none -> 82.1 us  [body(): pl.pallas_call(layer_kernel, out_shape=jax.ShapeDtypeStruct((B, COLS), BF...]
    all_to_all x2 -> x0, waiting for transfers between devices: 17 us -> none  [the longest x1 9.85 us: sent_and_summed(): lax.all_to_all(pieces, axis, split_axis=0, concat_axis=0, tiled=True)]
    all_to_all x2 -> x0, starting transfers between devices: 15 us -> none  [the longest x1 11.2 us: copy_for_each(): return lax.all_to_all(copies, axis, split_axis=0, concat_axis=0, tiled=True)]
    dot_general x8 -> x0, matrix products: 12.6 us -> none  [the longest x1 3.99 us: body(): jnp.einsum('rd,kdf->rkf', row_block, gate_up, preferred_element_type=jnp....]
    reshape x6 -> x0, local copies, waits for them, and re-layouts: 9.73 us -> none  [the longest x3 8.34 us: split_up(): x.reshape(*lengths[:dim], count, lengths[dim] // count, *lengths[dim + 1:])]
    reduce_sum x9 -> x0, other arithmetic: 2.65 us -> none  [the longest x2 1.28 us: sent_and_summed(): return arrived.astype(jnp.float32).sum(axis=0)]
  transfers between devices with their start and end apart: 2 -> 0, of which waited for: 2 -> 0; matrix products, arithmetic and copies ran while one was open for 1% -> 0% of each run, Pallas kernels for 0% -> 0%
where the time goes in v1:
time: 86.5 us; the launch traced here: 86.2 us
  Pallas kernels  82.1 us (95%)
  other arithmetic  2.68 us (3%)
  local copies, waits for them, and re-layouts  1.32 us (2%)
    pallas_call x1, Pallas kernels, body(): pl.pallas_call(layer_kernel, out_shape=jax.ShapeDtypeStruct((B, COLS), BF...  82.1 us

profile of v1, /device:TPU:1, one launch (start us, length us, event | category | flops | bytes accessed | tf_op | source)
XLA Modules:
  0.0 86.2 jit_solution(5317747795915969754)
XLA Ops:
  0.0 0.7 convert_element_type.3
  0.7 1.2 %pad_maximum_fusion.gains_hbm = f32[2,128]{1,0:T(2,128)} fusion(f32[1,128]{1,0:T(1,128)} %bitcast.2, f32[1,128]{1,0:T(1,128)} %bitcast.3), kind=kLoop, calls=%fused_computation.3 | loop fusion | flops 256 | bytes 2048 | tf_op jit(solution)/shard_map/stack | solution.py:341
  1.9 0.1 multiply_cosine_fusion
  2.0 0.7 maximum_maximum_fusion.tables_hbm
  2.7 82.1 %decoder_layer.1 = bf16[64,128]{1,0:T(8,128)(2,1)} custom-call(s32[10]{0:T(128)} %order_ref.1, s32[2]{0:T(128)} %len_ref.1, f32[4,128]{1,0:T(4,128)} %maximum_maximum_fusion.tables_hbm, bf16[64,128]{1,0:T(8,128)(2,1)} %tokens_hbm.1, f32[2,128]{1,0:T(2,128)} %pad_maximum_fusion.gains_hbm, bf16[128,2560]{1,0:T(8,128)(2,1)} %qkv_hbm.1, ...), custom_call_target="tpu_custom_call" | custom-call | tf_op jit(solution)/shard_map/decoder_layer/pallas_call | solution.py:344
  84.8 1.3 %copy.13 = bf16[64,128]{1,0:T(8,128)(2,1)} copy(bf16[64,128]{1,0:T(8,128)(2,1)} %decoder_layer.1) | data formatting | bytes 32768
  (1 shorter events, 0.0 us)

commit v2 on v1

--- a/solution.py
+++ b/solution.py
@@ -1,5 +1,6 @@
 import jax
 import jax.numpy as jnp
+import numpy as np
 from jax import lax
 from jax.experimental import pallas as pl
 from jax.experimental.pallas import tpu as pltpu
@@ -23,21 +24,23 @@
 SLOT_ROWS = 24
 LOCAL_HEADS = HEADS // TENSOR
 UNITS = FF // TENSOR
-ROW_BLOCKS = 4
-COL_BLOCKS = RANKS // ROW_BLOCKS
-ROWS_EACH = B // ROW_BLOCKS
-UNITS_EACH = UNITS // COL_BLOCKS
+SECTIONS = 8
+NX, NY, NZ = 4, 4, 2
+ROWS_EACH = B // NY
+UNITS_EACH = UNITS // SECTIONS
+CHUNKS = (("x", 0, 2), ("y", 2, 2), ("z", 4, 1), ("x", 5, 1), ("y", 6, 1))
 MESH = pl.DeviceIdType.MESH
 F32 = jnp.float32
 BF16 = jnp.bfloat16
 
 
 def layer_kernel(
-    order_ref,
-    len_ref,
-    tables_hbm,
+    order_hbm,
+    len_hbm,
+    freq_hbm,
     tokens_hbm,
-    gains_hbm,
+    gain1_hbm,
+    gain2_hbm,
     qkv_hbm,
     keys_hbm,
     values_hbm,
@@ -45,7 +48,9 @@
     gate_up_hbm,
     down_hbm,
     out_ref,
-    tables,
+    order_ref,
+    len_ref,
+    freq,
     tokens,
     gains,
     qkvw,
@@ -64,14 +69,13 @@
     proj2,
     sq_out,
     sq_in,
-    gu_out,
-    gu_in,
-    act,
-    load_sem,
-    send_sem,
-    recv_sem,
+    *rest_refs,
 ):
+    gu_out, gu_in1, gu_sum, gu_in2, act = (rest_refs[5 * i : 5 * i + 5] for i in range(5))
+    load_sem, send_sem, recv_sem = rest_refs[25:]
     section = lax.axis_index("section")
+    x = section // NZ
+    z = lax.rem(section, NZ)
     dp = lax.axis_index("dp")
     tensor = lax.axis_index("tensor")
     rank = section * DP + dp
@@ -81,14 +85,17 @@
 
     loads = [
         load(0, tokens_hbm, tokens),
-        load(1, gains_hbm, gains),
+        load(1, gain1_hbm, gains.at[0]),
         load(2, qkv_hbm, qkvw),
-        load(3, tables_hbm, tables),
+        load(3, freq_hbm, freq),
         load(4, keys_hbm, keys),
         load(5, values_hbm, values),
         load(6, outw_hbm, outw),
         load(7, gate_up_hbm, gate_up),
         load(8, down_hbm, down),
+        load(9, gain2_hbm, gains.at[1]),
+        load(10, order_hbm, order_ref),
+        load(11, len_hbm, len_ref),
     ]
     for copy in loads:
         copy.start()
@@ -120,7 +127,7 @@
         joined32[:, 20 + i, :] = part
         left = left - part
     joined32[:, 23, :] = jnp.zeros((B, HD), F32)
-    scaled = (wide * gains[0:1, :]).astype(BF16)
+    scaled = (wide * gains[0]).astype(BF16)
     loads[2].wait()
     for j in range(LOCAL_GROUPS * GROUP // 2):
         product = jnp.dot(scaled, qkvw[:, j * 256 : j * 256 + 256], preferred_element_type=F32)
@@ -133,6 +140,15 @@
         return carry
 
     lax.fori_loop(0, RANKS, pack, 0)
+    for i in (3, 9, 10, 11):
+        loads[i].wait()
+    low = lax.broadcasted_iota(jnp.int32, (1, HD), 1) < HD // 2
+    cosines, sines = [], []
+    for b in range(SEQS):
+        angle = freq[...] * len_ref[b].astype(F32)
+        cosines.append(jnp.cos(angle))
+        sine = jnp.sin(angle)
+        sines.append(jnp.where(low, -sine, sine))
     joined_in[rank] = joined_out[rank]
 
     pl.semaphore_wait(barrier, RANKS - 1 + TENSOR - 1)
@@ -166,7 +182,6 @@
     for i in range(1, RANKS):
         joined = joined + joined_in[i].astype(F32)
 
-    loads[3].wait()
     loads[4].wait()
     loads[5].wait()
     inv_scale = HD**-0.5
@@ -182,7 +197,7 @@
                 row = joined[base + g * GROUP + j : base + g * GROUP + j + 1]
                 logical = jnp.where(logical_row == order_ref[j], row, logical)
             logical = logical * factor
-            rotated = logical * tables[b : b + 1] + pltpu.roll(logical, HD // 2, 1) * tables[SEQS + b : SEQS + b + 1]
+            rotated = logical * cosines[b] + pltpu.roll(logical, HD // 2, 1) * sines[b]
             rotated = rotated.astype(BF16)
             queries = rotated[0:PER_GROUP]
             new_key = rotated.astype(F32)[PER_GROUP : PER_GROUP + 1]
@@ -220,14 +235,17 @@
     partial = jnp.dot(attended, outw[...], preferred_element_type=F32)
 
     def sum_over_tensor(value, buffer, i):
-        buffer[tensor] = value
+        buffer[tensor] = value.astype(BF16)
         for k in range(1, TENSOR):
             remote(buffer.at[tensor], buffer.at[tensor], i, tensor_peer(k)).start()
         others = pl.ds(0, TENSOR - 1)
         whole = remote(buffer.at[others], buffer.at[others], i, tensor_peer(1))
         whole.wait_send()
         whole.wait_recv()
-        return buffer[0] + buffer[1] + buffer[2] + buffer[3]
+        total = buffer[0].astype(F32)
+        for k in range(1, TENSOR):
+            total = total + buffer[k].astype(F32)
+        return total
 
     projected = sum_over_tensor(partial, proj1, 2)
     hidden = (tokens[...].astype(F32) + projected).astype(BF16).astype(F32)
@@ -244,77 +262,154 @@
         return carry
 
     lax.fori_loop(1, RANKS, send_squares, 0)
-    scaled = (hidden * gains[1:2, :]).astype(BF16)
+    scaled = (hidden * gains[1]).astype(BF16)
     loads[7].wait()
-    my_rows = rank // COL_BLOCKS
-    my_units = lax.rem(rank, COL_BLOCKS)
-
-    def block_of(a, c):
-        rows = pl.ds(pl.multiple_of(a * ROWS_EACH, ROWS_EACH), ROWS_EACH)
-        units = pl.ds(pl.multiple_of(c * UNITS_EACH, 128), UNITS_EACH)
-        return rows, units
-
-    def produce(i, carry):
-        c = lax.rem(my_units + i, COL_BLOCKS)
-        units = pl.ds(pl.multiple_of(c * UNITS_EACH, 128), UNITS_EACH)
-        for half in range(2):
-            product = jnp.dot(scaled, gate_up[half, :, units], preferred_element_type=F32)
-            gu_out[half, :, units] = product.astype(BF16)
-
-        def send_block(j, inner):
-            a = lax.rem(my_rows + j, ROW_BLOCKS)
-            other = a * COL_BLOCKS + c
-            rows, _ = block_of(a, c)
-
-            @pl.when(other != rank)
-            def _():
-                device = {"section": other // DP, "dp": lax.rem(other, DP)}
-                remote(gu_out.at[:, rows, units], gu_in.at[rank], 4, device).start()
-
-            return inner
-
-        lax.fori_loop(0, ROW_BLOCKS, send_block, 0)
-        return carry
-
-    lax.fori_loop(0, COL_BLOCKS, produce, 0)
-    rows, units = block_of(my_rows, my_units)
-    gu_in[rank] = gu_out[:, rows, units]
+
+    def at(dx, dy, dz):
+        x2, y2, z2 = lax.rem(x + dx, NX), lax.rem(dp + dy, NY), lax.rem(z + dz, NZ)
+        return x2, y2, z2, {"section": x2 * NZ + z2, "dp": y2}
+
+    def rows_of(y2):
+        return pl.ds(pl.multiple_of(y2 * ROWS_EACH, ROWS_EACH), ROWS_EACH)
+
+    own_rows = rows_of(dp)
+    first_peers = {
+        "x": [(2, 0, 0), (1, 0, 0), (3, 0, 0)],
+        "y": [(0, 2, 0), (0, 1, 0), (0, 3, 0)],
+        "z": [(0, 0, 1)],
+    }
+    second_peers = {
+        "x": [(0, dy, dz) for dy in (2, 1, 3, 0) for dz in (1, 0) if dy or dz],
+        "y": [(dx, 0, dz) for dx in (2, 1, 3, 0) for dz in (1, 0) if dx or dz],
+        "z": [(dx, dy, 0) for dx in (2, 1, 3, 0) for dy in (2, 1, 3, 0) if dx or dy],
+    }
+
+    def send(i, src, dst, device):
+        remote(src, dst, i, device).start()
+
+    def wait_recv(i, like):
+        remote(like, like, i, peer(1)[1]).wait_recv()
+
+    def wait_send(i, like):
+        remote(like, like, i, peer(1)[1]).wait_send()
+
+    base = 7
+    for p, (kind, first, count) in enumerate(CHUNKS):
+        out, arrived = gu_out[p], gu_in1[p]
+        width = count * 128
+        for c in range(SECTIONS):
+            for half in range(2):
+                start = c * UNITS_EACH + first * 128
+                product = jnp.dot(
+                    scaled, gate_up[half, :, start : start + width], preferred_element_type=F32
+                ).astype(BF16)
+                if kind == "x":
+                    out[c // NZ, c % NZ, half] = product
+                elif kind == "y":
+                    for y2 in range(NY):
+                        out[y2, c, half] = product[y2 * ROWS_EACH : (y2 + 1) * ROWS_EACH]
+                else:
+                    out[c % NZ, c // NZ, half] = product
+        for k, offset in enumerate(first_peers[kind]):
+            x2, y2, z2, device = at(*offset)
+            to = {"x": x2, "y": y2, "z": z2}[kind]
+            send(base + p, out.at[to], arrived.at[k], device)
+    for p, (kind, first, count) in enumerate(CHUNKS):
+        out, arrived, total, arrived2 = gu_out[p], gu_in1[p], gu_sum[p], gu_in2[p]
+        wait_recv(base + p, arrived)
+        mine = {"x": x, "y": dp, "z": z}[kind]
+
+        def add(i, carry):
+            for half in range(2):
+                value = out[mine, i, half].astype(F32)
+                for k in range(len(first_peers[kind])):
+                    value = value + arrived[k, i, half].astype(F32)
+                total[i, half] = value.astype(BF16)
+            return carry
+
+        lax.fori_loop(0, total.shape[0], add, 0)
+        for k, offset in enumerate(second_peers[kind]):
+            x2, y2, z2, device = at(*offset)
+            if kind == "x":
+                src = total.at[z2, :, rows_of(y2)]
+            elif kind == "y":
+                src = total.at[x2 * NZ + z2]
+            else:
+                src = total.at[x2, :, rows_of(y2)]
+            send(base + 5 + p, src, arrived2.at[k], device)
+
     wait_all(sq_in.at[rest], sq_in.at[rest], 3)
     total = jnp.sum(sq_in[...], axis=0)
-    mine = lax.broadcasted_iota(jnp.int32, (ROWS_EACH, HD), 0) + my_rows * ROWS_EACH
+    row_of = lax.broadcasted_iota(jnp.int32, (ROWS_EACH, HD), 0) + dp * ROWS_EACH
     lane_of = lax.broadcasted_iota(jnp.int32, (ROWS_EACH, HD), 1)
-    total = jnp.sum(jnp.where(mine == lane_of, total, 0.0), axis=1, keepdims=True)
+    total = jnp.sum(jnp.where(row_of == lane_of, total, 0.0), axis=1, keepdims=True)
     factor = lax.rsqrt(total / D + 1e-05)
-    wait_all(gu_in.at[rest], gu_in.at[rest], 4)
-    for j in range(UNITS_EACH // 128):
-        lanes = slice(j * 128, j * 128 + 128)
-
-        def add(i, sums):
-            return (
-                sums[0] + gu_in[i, 0, :, lanes].astype(F32),
-                sums[1] + gu_in[i, 1, :, lanes].astype(F32),
+
+    for p, (kind, first, count) in enumerate(CHUNKS):
+        total, arrived2, part = gu_sum[p], gu_in2[p], act[p]
+        wait_recv(base + 5 + p, arrived2)
+        halves = []
+        for half in range(2):
+            if kind == "x":
+                value = total[z, half, own_rows]
+            elif kind == "y":
+                value = total[section, half]
+            else:
+                value = total[x, half, own_rows]
+            value = value.astype(F32)
+            for k in range(len(second_peers[kind])):
+                value = value + arrived2[k, half].astype(F32)
+            halves.append(value * factor)
+        gate, up = halves
+        part[x, z, own_rows] = (gate / (1.0 + jnp.exp(-gate)) * up).astype(BF16)
+        block = part.at[x, z, own_rows]
+        for offset in second_peers[kind]:
+            send(base + 10 + p, block, block, at(*offset)[3])
+    for p, (kind, first, count) in enumerate(CHUNKS):
+        part = act[p]
+        wait_recv(base + 10 + p, gu_in2[p].at[:, 0])
+        if kind == "x":
+            block = part.at[x]
+        elif kind == "y":
+            block = part.at[:, :, own_rows]
+        else:
+            block = part.at[:, z]
+        for offset in first_peers[kind]:
+            send(base + 15 + p, block, block, at(*offset)[3])
+    loads[8].wait()
+    partial = jnp.zeros((B, COLS), F32)
+    for p, (kind, first, count) in enumerate(CHUNKS):
+        wait_recv(base + 15 + p, gu_in1[p].at[:, :, 0])
+        width = count * 128
+        for c in range(SECTIONS):
+            start = c * UNITS_EACH + first * 128
+            partial = partial + jnp.dot(
+                act[p][c // NZ, c % NZ], down[start : start + width], preferred_element_type=F32
             )
-
-        zero = jnp.zeros((ROWS_EACH, 128), F32)
-        gate, up = lax.fori_loop(0, RANKS, add, (zero, zero), unroll=8)
-        gate = gate * factor
-        up = up * factor
-        value = gate / (1.0 + jnp.exp(-gate)) * up
-        act[rows, pl.ds(pl.multiple_of(my_units * UNITS_EACH + j * 128, 128), 128)] = value.astype(BF16)
-
-    def send_activated(k, carry):
-        other, device = peer(k)
-        remote(act.at[rows, units], act.at[rows, units], 5, device).start()
-        return carry
-
-    lax.fori_loop(1, RANKS, send_activated, 0)
-    whole = remote(gu_in.at[rest, 0], gu_in.at[rest, 0], 5, peer(1)[1])
-    whole.wait_send()
-    whole.wait_recv()
-    loads[8].wait()
-    partial = jnp.dot(act[...], down[...], preferred_element_type=F32)
     lowered = sum_over_tensor(partial, proj2, 6)
-    out_ref[...] = (hidden + lowered).astype(BF16)
+    for p in range(5):
+        wait_send(base + p, gu_in1[p])
+        wait_send(base + 5 + p, gu_in2[p])
+        wait_send(base + 10 + p, gu_in2[p].at[:, 0])
+        wait_send(base + 15 + p, gu_in1[p].at[:, :, 0])
+    out_ref[...] = hidden + lowered
+
+
+def chunk_buffers():
+    out, in1, total, in2, act = [], [], [], [], []
+    for kind, first, count in CHUNKS:
+        w = count * 128
+        ways, block, peers = {
+            "x": (NX, (NZ, 2, B, w), 7),
+            "y": (NY, (SECTIONS, 2, ROWS_EACH, w), 7),
+            "z": (NZ, (NX, 2, B, w), 15),
+        }[kind]
+        out.append(pltpu.VMEM((ways, *block), BF16))
+        in1.append(pltpu.VMEM((ways - 1, *block), BF16))
+        total.append(pltpu.VMEM(block, BF16))
+        in2.append(pltpu.VMEM((peers, 2, ROWS_EACH, w), BF16))
+        act.append(pltpu.VMEM((NX, NZ, B, w), BF16))
+    return [*out, *in1, *total, *in2, *act]
 
 
 def body(
@@ -331,25 +426,20 @@
     down_weight,
 ):
     half_dim = HD // 2
-    inv_freq = 500000.0 ** (-(2.0 * jnp.arange(half_dim, dtype=F32)) / HD)
-    angles = cache_len.astype(F32)[:, None] * inv_freq[None, :]
-    cosine = jnp.cos(angles)
-    sine = jnp.sin(angles)
-    tables = jnp.concatenate(
-        [jnp.concatenate([cosine, cosine], axis=1), jnp.concatenate([-sine, sine], axis=1)], axis=0
-    )
-    gains = jnp.stack([attn_gain, ffn_gain])
-    smem = pl.BlockSpec(memory_space=pltpu.SMEM)
+    inv_freq = 500000.0 ** (-(2.0 * np.arange(half_dim)) / HD)
+    inv_freq = np.concatenate([inv_freq, inv_freq])[None, :].astype(np.float32)
     hbm = pl.BlockSpec(memory_space=pl.ANY)
-    return pl.pallas_call(
+    out = pl.pallas_call(
         layer_kernel,
-        out_shape=jax.ShapeDtypeStruct((B, COLS), BF16),
-        in_specs=[smem, smem] + [hbm] * 9,
+        out_shape=jax.ShapeDtypeStruct((B, COLS), F32),
+        in_specs=[hbm] * 12,
         out_specs=pl.BlockSpec(memory_space=pltpu.VMEM),
         scratch_shapes=[
-            pltpu.VMEM((2 * SEQS, HD), F32),
+            pltpu.SMEM((GROUP,), jnp.int32),
+            pltpu.SMEM((SEQS,), jnp.int32),
+            pltpu.VMEM((1, HD), F32),
             pltpu.VMEM((B, COLS), BF16),
-            pltpu.VMEM((2, COLS), F32),
+            pltpu.VMEM((2, 1, COLS), F32),
             pltpu.VMEM(qkv_weight.shape, BF16),
             pltpu.VMEM(cache_keys.shape, BF16),
             pltpu.VMEM(cache_values.shape, BF16),
@@ -362,16 +452,14 @@
             pltpu.VMEM((SEQS * LOCAL_HEADS, HD), F32),
             pltpu.VMEM((RANKS, SEQS * LOCAL_HEADS, HD), BF16),
             pltpu.VMEM((B, LOCAL_HEADS, HD), F32),
-            pltpu.VMEM((TENSOR, B, COLS), F32),
-            pltpu.VMEM((TENSOR, B, COLS), F32),
+            pltpu.VMEM((TENSOR, B, COLS), BF16),
+            pltpu.VMEM((TENSOR, B, COLS), BF16),
             pltpu.VMEM((1, 128), F32),
             pltpu.VMEM((RANKS, 1, 128), F32),
-            pltpu.VMEM((2, B, UNITS), BF16),
-            pltpu.VMEM((RANKS, 2, ROWS_EACH, UNITS_EACH), BF16),
-            pltpu.VMEM((B, UNITS), BF16),
-            pltpu.SemaphoreType.DMA((9,)),
-            pltpu.SemaphoreType.DMA((7,)),
-            pltpu.SemaphoreType.DMA((7,)),
+            *chunk_buffers(),
+            pltpu.SemaphoreType.DMA((12,)),
+            pltpu.SemaphoreType.DMA((27,)),
+            pltpu.SemaphoreType.DMA((27,)),
         ],
         compiler_params=pltpu.CompilerParams(
             collective_id=0, has_side_effects=True, vmem_limit_bytes=60 * 2**20
@@ -380,9 +468,10 @@
     )(
         qkv_order,
         cache_len,
-        tables,
+        inv_freq,
         tokens,
-        gains,
+        attn_gain.reshape(1, COLS),
+        ffn_gain.reshape(1, COLS),
         qkv_weight,
         cache_keys,
         cache_values,
@@ -390,6 +479,7 @@
         gate_up,
         down_weight,
     )
+    return out.astype(BF16)
 
 
 def solution(mesh):

time: 86.5 us -> 64.1 us (0.74)
  Pallas kernels: 82.1 us -> 62.5 us
  local copies, waits for them, and re-layouts: 1.32 us -> 0 us
  other arithmetic: 2.68 us -> 1.37 us
    pallas_call x1, Pallas kernels: 82.1 us -> 62.5 us  [body(): pl.pallas_call(layer_kernel, out_shape=jax.ShapeDtypeStruct((B, COLS), F3...]
    unnamed x1 -> x0, local copies, waits for them, and re-layouts: 1.32 us -> none
    another operation x1 -> x0, other arithmetic: 1.24 us -> none  [body(): gains = jnp.stack([attn_gain, ffn_gain])]
where the time goes in v2:
time: 64.1 us; the launch traced here: 63.9 us
  Pallas kernels  62.5 us (98%)
  other arithmetic  1.37 us (2%)
    pallas_call x1, Pallas kernels, body(): pl.pallas_call(layer_kernel, out_shape=jax.ShapeDtypeStruct((B, COLS), F3...  62.5 us
    convert_element_type x1, other arithmetic, body(): return out.astype(BF16)  1.37 us

profile of v2, /device:TPU:1, one launch (start us, length us, event | category | flops | bytes accessed | tf_op | source)
XLA Modules:
  0.0 63.9 jit_solution(17496926815396953989)
XLA Ops:
  0.0 62.5 %decoder_layer.1 = f32[64,128]{1,0:T(8,128)} custom-call(s32[10]{0:T(128)} %order_hbm.1, s32[2]{0:T(128)} %len_hbm.1, f32[1,128]{1,0:T(1,128)} %constant.2.clone.freq_hbm, bf16[64,128]{1,0:T(8,128)(2,1)} %tokens_hbm.1, f32[1,128]{1,0:T(1,128)} %bitcast.2, f32[1,128]{1,0:T(1,128)} %bitcast.3, bf16[128,2560]{1,0:T(8,128)(2,1)} %qkv_hbm.1, ...), custom_call_target="tpu_custom_call" | custom-call | tf_op jit(solution)/shard_map/decoder_layer/pallas_call | solution.py:432
  62.5 1.4 %convert_element_type.3 = bf16[64,128]{1,0:T(8,128)(2,1)} convert(f32[64,128]{1,0:T(8,128)} %decoder_layer.1) | non-fusion elementwise | flops 8192 | bytes 49152 | tf_op jit(solution)/shard_map/convert_element_type | solution.py:482

commit v3 on v2

--- a/solution.py
+++ b/solution.py
@@ -28,6 +28,10 @@
 NX, NY, NZ = 4, 4, 2
 ROWS_EACH = B // NY
 UNITS_EACH = UNITS // SECTIONS
+FAR_FIRST = sorted(
+    [(dx, dy, dz) for dx in range(NX) for dy in range(NY) for dz in range(NZ) if dx or dy or dz],
+    key=lambda o: -(min(o[0], NX - o[0]) + min(o[1], NY - o[1]) + 2 * o[2]),
+)
 CHUNKS = (("x", 0, 2), ("y", 2, 2), ("z", 4, 1), ("x", 5, 1), ("y", 6, 1))
 MESH = pl.DeviceIdType.MESH
 F32 = jnp.float32
@@ -71,8 +75,8 @@
     sq_in,
     *rest_refs,
 ):
-    gu_out, gu_in1, gu_sum, gu_in2, act = (rest_refs[5 * i : 5 * i + 5] for i in range(5))
-    load_sem, send_sem, recv_sem = rest_refs[25:]
+    gu_out, gu_in1, gu_passed, gu_sum, gu_in2, act = (rest_refs[5 * i : 5 * i + 5] for i in range(6))
+    lowered_sum, load_sem, send_sem, recv_sem = rest_refs[30:]
     section = lax.axis_index("section")
     x = section // NZ
     z = lax.rem(section, NZ)
@@ -97,25 +101,26 @@
         load(10, order_hbm, order_ref),
         load(11, len_hbm, len_ref),
     ]
+    def at(dx, dy, dz):
+        x2, y2, z2 = lax.rem(x + dx, NX), lax.rem(dp + dy, NY), lax.rem(z + dz, NZ)
+        return x2, y2, z2, {"section": x2 * NZ + z2, "dp": y2}
+
+    def peer(offset):
+        x2, y2, z2, device = at(*offset)
+        return (x2 * NZ + z2) * DP + y2, device
+
+    def tensor_peer(k):
+        return {"tensor": lax.rem(tensor + k, TENSOR)}
+
+    barrier = pltpu.get_barrier_semaphore()
+
+    for offset in FAR_FIRST:
+        pl.semaphore_signal(barrier, inc=1, device_id=peer(offset)[1], device_id_type=MESH)
+    for k in range(1, TENSOR):
+        pl.semaphore_signal(barrier, inc=1, device_id=tensor_peer(k), device_id_type=MESH)
+
     for copy in loads:
         copy.start()
-
-    def peer(k):
-        other = lax.rem(rank + k, RANKS)
-        return other, {"section": other // DP, "dp": lax.rem(other, DP)}
-
-    def tensor_peer(k):
-        return {"tensor": lax.rem(tensor + k, TENSOR)}
-
-    barrier = pltpu.get_barrier_semaphore()
-
-    def greet(k, carry):
-        pl.semaphore_signal(barrier, inc=1, device_id=peer(k)[1], device_id_type=MESH)
-        return carry
-
-    lax.fori_loop(1, RANKS, greet, 0)
-    for k in range(1, TENSOR):
-        pl.semaphore_signal(barrier, inc=1, device_id=tensor_peer(k), device_id_type=MESH)
 
     loads[0].wait()
     loads[1].wait()
@@ -124,19 +129,18 @@
     left = jnp.broadcast_to(squares, (B, HD))
     for i in range(3):
         part = left.astype(BF16).astype(F32)
-        joined32[:, 20 + i, :] = part
+        joined32[pl.Slice(20 + i, B, SLOT_ROWS)] = part
         left = left - part
-    joined32[:, 23, :] = jnp.zeros((B, HD), F32)
+    joined32[pl.Slice(23, B, SLOT_ROWS)] = jnp.zeros((B, HD), F32)
     scaled = (wide * gains[0]).astype(BF16)
     loads[2].wait()
     for j in range(LOCAL_GROUPS * GROUP // 2):
         product = jnp.dot(scaled, qkvw[:, j * 256 : j * 256 + 256], preferred_element_type=F32)
-        joined32[:, 2 * j, :] = product[:, :HD]
-        joined32[:, 2 * j + 1, :] = product[:, HD:]
+        joined32[pl.Slice(2 * j, B, SLOT_ROWS)] = product[:, :HD]
+        joined32[pl.Slice(2 * j + 1, B, SLOT_ROWS)] = product[:, HD:]
 
     def pack(i, carry):
-        rows = joined32[pl.ds(i * SEQS, SEQS)]
-        joined_out[i] = rows.reshape(SEQS * SLOT_ROWS, HD).astype(BF16)
+        joined_out[i] = joined32[pl.ds(i * SEQS * SLOT_ROWS, SEQS * SLOT_ROWS)].astype(BF16)
         return carry
 
     lax.fori_loop(0, RANKS, pack, 0)
@@ -163,15 +167,12 @@
             device_id_type=MESH,
         )
 
-    def send_joined(k, carry):
-        other, device = peer(k)
+    for offset in FAR_FIRST:
+        other, device = peer(offset)
         remote(joined_out.at[other], joined_in.at[rank], 0, device).start()
-        return carry
-
-    lax.fori_loop(1, RANKS, send_joined, 0)
 
     def wait_all(src, dst, i):
-        whole = remote(src, dst, i, peer(1)[1])
+        whole = remote(src, dst, i, peer(FAR_FIRST[-1])[1])
         whole.wait_send()
         whole.wait_recv()
 
@@ -217,21 +218,17 @@
 
     att_in[rank] = att_out[...].astype(BF16)
 
-    def send_attended(k, carry):
-        other, device = peer(k)
-        remote(att_in.at[rank], att_in.at[rank], 1, device).start()
-        return carry
-
-    lax.fori_loop(1, RANKS, send_attended, 0)
+    for offset in FAR_FIRST:
+        remote(att_in.at[rank], att_in.at[rank], 1, peer(offset)[1]).start()
     wait_all(att_in.at[rest], att_in.at[rest], 1)
 
     def widen(i, carry):
-        att32[pl.ds(i * SEQS, SEQS)] = att_in[i].astype(F32).reshape(SEQS, LOCAL_HEADS, HD)
+        att32[pl.ds(i * SEQS * LOCAL_HEADS, SEQS * LOCAL_HEADS)] = att_in[i].astype(F32)
         return carry
 
     lax.fori_loop(0, RANKS, widen, 0)
     loads[6].wait()
-    attended = jnp.concatenate([att32[:, h, :].astype(BF16) for h in range(LOCAL_HEADS)], axis=1)
+    attended = jnp.concatenate([att32[pl.Slice(h, B, LOCAL_HEADS)].astype(BF16) for h in range(LOCAL_HEADS)], axis=1)
     partial = jnp.dot(attended, outw[...], preferred_element_type=F32)
 
     def sum_over_tensor(value, buffer, i):
@@ -256,23 +253,16 @@
     sq_out[...] = jnp.sum(jnp.where(row_of == lane_of, squares, 0.0), axis=0, keepdims=True)
     sq_in[rank] = sq_out[...]
 
-    def send_squares(k, carry):
-        other, device = peer(k)
-        remote(sq_out, sq_in.at[rank], 3, device).start()
-        return carry
-
-    lax.fori_loop(1, RANKS, send_squares, 0)
+    for offset in FAR_FIRST:
+        remote(sq_out, sq_in.at[rank], 3, peer(offset)[1]).start()
     scaled = (hidden * gains[1]).astype(BF16)
     loads[7].wait()
 
-    def at(dx, dy, dz):
-        x2, y2, z2 = lax.rem(x + dx, NX), lax.rem(dp + dy, NY), lax.rem(z + dz, NZ)
-        return x2, y2, z2, {"section": x2 * NZ + z2, "dp": y2}
-
     def rows_of(y2):
         return pl.ds(pl.multiple_of(y2 * ROWS_EACH, ROWS_EACH), ROWS_EACH)
 
     own_rows = rows_of(dp)
+    ring = {"x": [(1, 0, 0), (3, 0, 0), (2, 0, 0)], "y": [(0, 1, 0), (0, 3, 0), (0, 2, 0)]}
     first_peers = {
         "x": [(2, 0, 0), (1, 0, 0), (3, 0, 0)],
         "y": [(0, 2, 0), (0, 1, 0), (0, 3, 0)],
@@ -288,12 +278,13 @@
         remote(src, dst, i, device).start()
 
     def wait_recv(i, like):
-        remote(like, like, i, peer(1)[1]).wait_recv()
+        remote(like, like, i, peer(FAR_FIRST[-1])[1]).wait_recv()
 
     def wait_send(i, like):
-        remote(like, like, i, peer(1)[1]).wait_send()
+        remote(like, like, i, peer(FAR_FIRST[-1])[1]).wait_send()
 
     base = 7
+    step_a, step_b, step_c, step_2, step_3, step_4 = (base + 5 * i for i in range(6))
     for p, (kind, first, count) in enumerate(CHUNKS):
         out, arrived = gu_out[p], gu_in1[p]
         width = count * 128
@@ -307,36 +298,68 @@
                     out[c // NZ, c % NZ, half] = product
                 elif kind == "y":
                     for y2 in range(NY):
-                        out[y2, c, half] = product[y2 * ROWS_EACH : (y2 + 1) * ROWS_EACH]
+                        out[y2, c // 4, c % 4, half] = product[y2 * ROWS_EACH : (y2 + 1) * ROWS_EACH]
                 else:
                     out[c % NZ, c // NZ, half] = product
-        for k, offset in enumerate(first_peers[kind]):
-            x2, y2, z2, device = at(*offset)
-            to = {"x": x2, "y": y2, "z": z2}[kind]
-            send(base + p, out.at[to], arrived.at[k], device)
+        if kind == "z":
+            _, _, z2, device = at(0, 0, 1)
+            send(step_a + p, out.at[z2], arrived.at[0], device)
+            continue
+        along = 0 if kind == "x" else 1
+        after, before, across = ring[kind]
+        far, right, left = at(*across)[along], at(*after), at(*before)
+        send(step_a + p, out.at[far, 0], arrived.at[0, 0], right[3])
+        send(step_a + p, out.at[far, 1], arrived.at[0, 1], left[3])
+        send(step_b + p, out.at[right[along], 1], arrived.at[1, 1], right[3])
+        send(step_b + p, out.at[left[along], 0], arrived.at[1, 0], left[3])
+    for p, (kind, first, count) in enumerate(CHUNKS):
+        if kind == "z":
+            continue
+        out, arrived = gu_out[p], gu_in1[p]
+        along = 0 if kind == "x" else 1
+        after, before, _ = ring[kind]
+        right, left = at(*after), at(*before)
+        wait_recv(step_a + p, arrived.at[0])
+        passed = gu_passed[p]
+        for i, (to, device) in enumerate(((right[along], right[3]), (left[along], left[3]))):
+
+            def merge(j, carry):
+                passed[i, j] = (out[to, i, j].astype(F32) + arrived[0, i, j].astype(F32)).astype(BF16)
+                return carry
+
+            lax.fori_loop(0, passed.shape[1], merge, 0, unroll=True)
+            send(step_c + p, passed.at[i], arrived.at[2, i], device)
     for p, (kind, first, count) in enumerate(CHUNKS):
         out, arrived, total, arrived2 = gu_out[p], gu_in1[p], gu_sum[p], gu_in2[p]
-        wait_recv(base + p, arrived)
-        mine = {"x": x, "y": dp, "z": z}[kind]
-
-        def add(i, carry):
-            for half in range(2):
-                value = out[mine, i, half].astype(F32)
-                for k in range(len(first_peers[kind])):
-                    value = value + arrived[k, i, half].astype(F32)
-                total[i, half] = value.astype(BF16)
-            return carry
-
-        lax.fori_loop(0, total.shape[0], add, 0)
+        if kind == "z":
+            wait_recv(step_a + p, arrived)
+
+            def add(i, carry):
+                total[i] = (out[z, i].astype(F32) + arrived[0, i].astype(F32)).astype(BF16)
+                return carry
+
+            lax.fori_loop(0, total.shape[0], add, 0)
+        else:
+            wait_recv(step_b + p, arrived.at[1])
+            wait_recv(step_c + p, arrived.at[2])
+            mine = x if kind == "x" else dp
+            for i in range(2):
+
+                def add(j, carry):
+                    value = out[mine, i, j].astype(F32) + arrived[1, i, j].astype(F32)
+                    total[i, j] = (value + arrived[2, i, j].astype(F32)).astype(BF16)
+                    return carry
+
+                lax.fori_loop(0, total.shape[1], add, 0, unroll=True)
         for k, offset in enumerate(second_peers[kind]):
             x2, y2, z2, device = at(*offset)
             if kind == "x":
                 src = total.at[z2, :, rows_of(y2)]
             elif kind == "y":
-                src = total.at[x2 * NZ + z2]
+                src = total.at[x2 // 2, lax.rem(x2, 2) * NZ + z2]
             else:
                 src = total.at[x2, :, rows_of(y2)]
-            send(base + 5 + p, src, arrived2.at[k], device)
+            send(step_2 + p, src, arrived2.at[k], device)
 
     wait_all(sq_in.at[rest], sq_in.at[rest], 3)
     total = jnp.sum(sq_in[...], axis=0)
@@ -345,15 +368,22 @@
     total = jnp.sum(jnp.where(row_of == lane_of, total, 0.0), axis=1, keepdims=True)
     factor = lax.rsqrt(total / D + 1e-05)
 
-    for p, (kind, first, count) in enumerate(CHUNKS):
+    def like_3(p):
+        return gu_in2[p].at[:, 0]
+
+    def like_4(p):
+        return gu_in1[p].at[0, :, 0] if CHUNKS[p][0] == "z" else gu_in1[p].at[:, 0]
+
+    def activate(p):
+        kind = CHUNKS[p][0]
         total, arrived2, part = gu_sum[p], gu_in2[p], act[p]
-        wait_recv(base + 5 + p, arrived2)
+        wait_recv(step_2 + p, arrived2)
         halves = []
         for half in range(2):
             if kind == "x":
                 value = total[z, half, own_rows]
             elif kind == "y":
-                value = total[section, half]
+                value = total[x // 2, lax.rem(x, 2) * NZ + z, half]
             else:
                 value = total[x, half, own_rows]
             value = value.astype(F32)
@@ -364,10 +394,12 @@
         part[x, z, own_rows] = (gate / (1.0 + jnp.exp(-gate)) * up).astype(BF16)
         block = part.at[x, z, own_rows]
         for offset in second_peers[kind]:
-            send(base + 10 + p, block, block, at(*offset)[3])
-    for p, (kind, first, count) in enumerate(CHUNKS):
+            send(step_3 + p, block, block, at(*offset)[3])
+
+    def pass_on(p):
+        kind = CHUNKS[p][0]
         part = act[p]
-        wait_recv(base + 10 + p, gu_in2[p].at[:, 0])
+        wait_recv(step_3 + p, like_3(p))
         if kind == "x":
             block = part.at[x]
         elif kind == "y":
@@ -375,41 +407,59 @@
         else:
             block = part.at[:, z]
         for offset in first_peers[kind]:
-            send(base + 15 + p, block, block, at(*offset)[3])
-    loads[8].wait()
-    partial = jnp.zeros((B, COLS), F32)
-    for p, (kind, first, count) in enumerate(CHUNKS):
-        wait_recv(base + 15 + p, gu_in1[p].at[:, :, 0])
+            send(step_4 + p, block, block, at(*offset)[3])
+
+    def lower(p):
+        kind, first, count = CHUNKS[p]
+        wait_recv(step_4 + p, like_4(p))
         width = count * 128
+        partial = None
         for c in range(SECTIONS):
             start = c * UNITS_EACH + first * 128
-            partial = partial + jnp.dot(
+            product = jnp.dot(
                 act[p][c // NZ, c % NZ], down[start : start + width], preferred_element_type=F32
             )
+            partial = product if partial is None else partial + product
+        lowered_sum[...] = partial if p == 0 else lowered_sum[...] + partial
+
+    for p in range(5):
+        activate(p)
+    for p in range(5):
+        pass_on(p)
+    loads[8].wait()
+    for p in range(5):
+        lower(p)
+    partial = lowered_sum[...]
     lowered = sum_over_tensor(partial, proj2, 6)
     for p in range(5):
-        wait_send(base + p, gu_in1[p])
-        wait_send(base + 5 + p, gu_in2[p])
-        wait_send(base + 10 + p, gu_in2[p].at[:, 0])
-        wait_send(base + 15 + p, gu_in1[p].at[:, :, 0])
+        if CHUNKS[p][0] == "z":
+            wait_send(step_a + p, gu_in1[p])
+        else:
+            for i, step in enumerate((step_a, step_b, step_c)):
+                wait_send(step + p, gu_in1[p].at[i])
+        wait_send(step_2 + p, gu_in2[p])
+        wait_send(step_3 + p, like_3(p))
+        wait_send(step_4 + p, like_4(p))
     out_ref[...] = hidden + lowered
 
 
 def chunk_buffers():
-    out, in1, total, in2, act = [], [], [], [], []
+    out, in1, passed, total, in2, act = [], [], [], [], [], []
     for kind, first, count in CHUNKS:
         w = count * 128
-        ways, block, peers = {
-            "x": (NX, (NZ, 2, B, w), 7),
-            "y": (NY, (SECTIONS, 2, ROWS_EACH, w), 7),
-            "z": (NZ, (NX, 2, B, w), 15),
-        }[kind]
-        out.append(pltpu.VMEM((ways, *block), BF16))
-        in1.append(pltpu.VMEM((ways - 1, *block), BF16))
-        total.append(pltpu.VMEM(block, BF16))
+        if kind == "z":
+            shape, arrived, peers = (NX, 2, B, w), (1, NX, 2, B, w), NX * NY - 1
+            kept = (8, w)
+        else:
+            shape = {"x": (2, 2, B, w), "y": (2, 4, 2, ROWS_EACH, w)}[kind]
+            arrived, kept, peers = (3, *shape), shape, 7
+        out.append(pltpu.VMEM(({"x": NX, "y": NY, "z": NZ}[kind], *shape), BF16))
+        in1.append(pltpu.VMEM(arrived, BF16))
+        passed.append(pltpu.VMEM(kept, BF16))
+        total.append(pltpu.VMEM(shape, BF16))
         in2.append(pltpu.VMEM((peers, 2, ROWS_EACH, w), BF16))
         act.append(pltpu.VMEM((NX, NZ, B, w), BF16))
-    return [*out, *in1, *total, *in2, *act]
+    return [*out, *in1, *passed, *total, *in2, *act, pltpu.VMEM((B, COLS), F32)]
 
 
 def body(
@@ -446,38 +496,43 @@
             pltpu.VMEM(out_weight.shape, BF16),
             pltpu.VMEM(gate_up.shape, BF16),
             pltpu.VMEM(down_weight.shape, BF16),
-            pltpu.VMEM((B, SLOT_ROWS, HD), F32),
+            pltpu.VMEM((B * SLOT_ROWS, HD), F32),
             pltpu.VMEM((RANKS, SEQS * SLOT_ROWS, HD), BF16),
             pltpu.VMEM((RANKS, SEQS * SLOT_ROWS, HD), BF16),
             pltpu.VMEM((SEQS * LOCAL_HEADS, HD), F32),
             pltpu.VMEM((RANKS, SEQS * LOCAL_HEADS, HD), BF16),
-            pltpu.VMEM((B, LOCAL_HEADS, HD), F32),
+            pltpu.VMEM((B * LOCAL_HEADS, HD), F32),
             pltpu.VMEM((TENSOR, B, COLS), BF16),
             pltpu.VMEM((TENSOR, B, COLS), BF16),
             pltpu.VMEM((1, 128), F32),
             pltpu.VMEM((RANKS, 1, 128), F32),
             *chunk_buffers(),
             pltpu.SemaphoreType.DMA((12,)),
-            pltpu.SemaphoreType.DMA((27,)),
-            pltpu.SemaphoreType.DMA((27,)),
+            pltpu.SemaphoreType.DMA((37,)),
+            pltpu.SemaphoreType.DMA((37,)),
         ],
         compiler_params=pltpu.CompilerParams(
-            collective_id=0, has_side_effects=True, vmem_limit_bytes=60 * 2**20
+            collective_id=0, has_side_effects=True, vmem_limit_bytes=32 * 2**20
         ),
         name="decoder_layer",
     )(
-        qkv_order,
-        cache_len,
-        inv_freq,
-        tokens,
-        attn_gain.reshape(1, COLS),
-        ffn_gain.reshape(1, COLS),
-        qkv_weight,
-        cache_keys,
-        cache_values,
-        out_weight,
-        gate_up,
-        down_weight,
+        *(
+            pltpu.with_memory_space_constraint(operand, pltpu.HBM)
+            for operand in (
+                qkv_order,
+                cache_len,
+                jnp.asarray(inv_freq),
+                tokens,
+                attn_gain.reshape(1, COLS),
+                ffn_gain.reshape(1, COLS),
+                qkv_weight,
+                cache_keys,
+                cache_values,
+                out_weight,
+                gate_up,
+                down_weight,
+            )
+        )
     )
     return out.astype(BF16)
 

time: 64.1 us -> 60.4 us (0.942)
  Pallas kernels: 62.5 us -> 59.6 us
  other arithmetic: 1.37 us -> 0.61 us
    pallas_call x1, Pallas kernels: 62.5 us -> 59.6 us  [body(): pl.pallas_call(layer_kernel, out_shape=jax.ShapeDtypeStruct((B, COLS), F3...]
    convert_element_type x1, other arithmetic: 1.37 us -> 0.61 us  [body(): return out.astype(BF16)]
where the time goes in v3:
time: 60.4 us; the launch traced here: 60.2 us
  Pallas kernels  59.6 us (99%)
  other arithmetic  0.61 us (1%)
    pallas_call x1, Pallas kernels, body(): pl.pallas_call(layer_kernel, out_shape=jax.ShapeDtypeStruct((B, COLS), F3...  59.6 us

profile of v3, /device:TPU:1, one launch (start us, length us, event | category | flops | bytes accessed | tf_op | source)
XLA Modules:
  0.0 60.2 jit_solution(17668419106489472679)
XLA Ops:
  0.0 59.6 %decoder_layer.1 = f32[64,128]{1,0:T(8,128)S(1)} custom-call(s32[10]{0:T(128)} %order_hbm.1, s32[2]{0:T(128)} %len_hbm.1, f32[1,128]{1,0:T(1,128)} %constant.2.clone.freq_hbm, bf16[64,128]{1,0:T(8,128)(2,1)} %tokens_hbm.1, f32[1,128]{1,0:T(1,128)} %bitcast.2, f32[1,128]{1,0:T(1,128)} %bitcast.3, bf16[128,2560]{1,0:T(8,128)(2,1)} %qkv_hbm.1, ...), custom_call_target="tpu_custom_call" | custom-call | tf_op jit(solution)/shard_map/decoder_layer/pallas_call | solution.py:482
  59.6 0.6 %convert_element_type.3 = bf16[64,128]{1,0:T(8,128)(2,1)} convert(f32[64,128]{1,0:T(8,128)S(1)} %decoder_layer.1) | non-fusion elementwise | flops 8192 | bytes 49152 | tf_op jit(solution)/shard_map/convert_element_type | solution.py:537

commit v4 on v3

--- a/solution.py
+++ b/solution.py
@@ -32,7 +32,10 @@
     [(dx, dy, dz) for dx in range(NX) for dy in range(NY) for dz in range(NZ) if dx or dy or dz],
     key=lambda o: -(min(o[0], NX - o[0]) + min(o[1], NY - o[1]) + 2 * o[2]),
 )
-CHUNKS = (("x", 0, 2), ("y", 2, 2), ("z", 4, 1), ("x", 5, 1), ("y", 6, 1))
+CHUNKS = (("x", 0, 3), ("y", 3, 2), ("z", 5, 2))
+N_CHUNKS = len(CHUNKS)
+WAYS = {"x": NX, "y": NY, "z": NZ}
+BATCHES = {"x": (6, 4, 2), "y": (6, 4, 2), "z": (4, 2, 2)}
 MESH = pl.DeviceIdType.MESH
 F32 = jnp.float32
 BF16 = jnp.bfloat16
@@ -61,7 +64,6 @@
     keys,
     values,
     outw,
-    gate_up,
     down,
     joined32,
     joined_out,
@@ -75,8 +77,8 @@
     sq_in,
     *rest_refs,
 ):
-    gu_out, gu_in1, gu_passed, gu_sum, gu_in2, act = (rest_refs[5 * i : 5 * i + 5] for i in range(6))
-    lowered_sum, load_sem, send_sem, recv_sem = rest_refs[30:]
+    wide_weights, wide_rows, gu_sum, gu_in2, act = (rest_refs[N_CHUNKS * i : N_CHUNKS * (i + 1)] for i in range(5))
+    lowered_sum, own_rows_sem, load_sem, send_sem, recv_sem = rest_refs[5 * N_CHUNKS :]
     section = lax.axis_index("section")
     x = section // NZ
     z = lax.rem(section, NZ)
@@ -87,20 +89,19 @@
     def load(i, src, dst):
         return pltpu.make_async_copy(src, dst, load_sem.at[i])
 
-    loads = [
-        load(0, tokens_hbm, tokens),
-        load(1, gain1_hbm, gains.at[0]),
-        load(2, qkv_hbm, qkvw),
-        load(3, freq_hbm, freq),
-        load(4, keys_hbm, keys),
-        load(5, values_hbm, values),
-        load(6, outw_hbm, outw),
-        load(7, gate_up_hbm, gate_up),
-        load(8, down_hbm, down),
-        load(9, gain2_hbm, gains.at[1]),
-        load(10, order_hbm, order_ref),
-        load(11, len_hbm, len_ref),
-    ]
+    loads = {
+        0: load(0, tokens_hbm, tokens),
+        1: load(1, gain1_hbm, gains.at[0]),
+        2: load(2, qkv_hbm, qkvw),
+        3: load(3, freq_hbm, freq),
+        9: load(9, gain2_hbm, gains.at[1]),
+        10: load(10, order_hbm, order_ref),
+        11: load(11, len_hbm, len_ref),
+        4: load(4, keys_hbm, keys),
+        5: load(5, values_hbm, values),
+        6: load(6, outw_hbm, outw),
+        8: load(8, down_hbm, down),
+    }
     def at(dx, dy, dz):
         x2, y2, z2 = lax.rem(x + dx, NX), lax.rem(dp + dy, NY), lax.rem(z + dz, NZ)
         return x2, y2, z2, {"section": x2 * NZ + z2, "dp": y2}
@@ -119,7 +120,7 @@
     for k in range(1, TENSOR):
         pl.semaphore_signal(barrier, inc=1, device_id=tensor_peer(k), device_id_type=MESH)
 
-    for copy in loads:
+    for copy in loads.values():
         copy.start()
 
     loads[0].wait()
@@ -167,9 +168,47 @@
             device_id_type=MESH,
         )
 
+    ring = {
+        "x": [(2, 0, 0), (1, 0, 0), (3, 0, 0)],
+        "y": [(0, 2, 0), (0, 1, 0), (0, 3, 0)],
+        "z": [(0, 0, 1)],
+    }
+
+    def block_start(p, major, minor):
+        return pl.multiple_of((major * NZ + minor) * UNITS_EACH + CHUNKS[p][1] * 128, 128)
+
+    def weight_piece(p, to, i, half):
+        kind, _, count = CHUNKS[p]
+        start = block_start(p, i, to) if kind == "z" else block_start(p, to, i)
+        return gate_up_hbm.at[half, :, pl.ds(start, count * 128)]
+
+    def step_of(offset):
+        return max(offset)
+
+    place = {"x": x, "y": dp, "z": z}
+    pieces = {}
+    for p, (kind, _, _) in enumerate(CHUNKS):
+        pieces[p] = [
+            (offset, i, half) for i in range(NX if kind == "z" else NZ) for half in range(2) for offset in ring[kind]
+        ]
+        for i in range(NX if kind == "z" else NZ):
+            for half in range(2):
+                pltpu.make_async_copy(
+                    weight_piece(p, place[kind], i, half), wide_weights[p].at[i, half, pl.ds(0, 128)], own_rows_sem.at[p]
+                ).start()
+
+    def send_weights(batch):
+        for p, (kind, _, _) in enumerate(CHUNKS):
+            first = sum(BATCHES[kind][:batch])
+            for offset, i, half in pieces[p][first : first + BATCHES[kind][batch]]:
+                to = at(*offset)
+                dst = wide_weights[p].at[i, half, pl.ds(step_of(offset) * 128, 128)]
+                remote(weight_piece(p, to["xyz".index(kind)], i, half), dst, 7 + p, to[3]).start()
+
     for offset in FAR_FIRST:
         other, device = peer(offset)
         remote(joined_out.at[other], joined_in.at[rank], 0, device).start()
+    send_weights(0)
 
     def wait_all(src, dst, i):
         whole = remote(src, dst, i, peer(FAR_FIRST[-1])[1])
@@ -220,6 +259,7 @@
 
     for offset in FAR_FIRST:
         remote(att_in.at[rank], att_in.at[rank], 1, peer(offset)[1]).start()
+    send_weights(1)
     wait_all(att_in.at[rest], att_in.at[rest], 1)
 
     def widen(i, carry):
@@ -231,10 +271,11 @@
     attended = jnp.concatenate([att32[pl.Slice(h, B, LOCAL_HEADS)].astype(BF16) for h in range(LOCAL_HEADS)], axis=1)
     partial = jnp.dot(attended, outw[...], preferred_element_type=F32)
 
-    def sum_over_tensor(value, buffer, i):
+    def sum_over_tensor(value, buffer, i, then=lambda: None):
         buffer[tensor] = value.astype(BF16)
         for k in range(1, TENSOR):
             remote(buffer.at[tensor], buffer.at[tensor], i, tensor_peer(k)).start()
+        then()
         others = pl.ds(0, TENSOR - 1)
         whole = remote(buffer.at[others], buffer.at[others], i, tensor_peer(1))
         whole.wait_send()
@@ -244,7 +285,7 @@
             total = total + buffer[k].astype(F32)
         return total
 
-    projected = sum_over_tensor(partial, proj1, 2)
+    projected = sum_over_tensor(partial, proj1, 2, lambda: send_weights(2))
     hidden = (tokens[...].astype(F32) + projected).astype(BF16).astype(F32)
 
     squares = jnp.sum(hidden * hidden, axis=1, keepdims=True)
@@ -253,21 +294,10 @@
     sq_out[...] = jnp.sum(jnp.where(row_of == lane_of, squares, 0.0), axis=0, keepdims=True)
     sq_in[rank] = sq_out[...]
 
-    for offset in FAR_FIRST:
-        remote(sq_out, sq_in.at[rank], 3, peer(offset)[1]).start()
     scaled = (hidden * gains[1]).astype(BF16)
-    loads[7].wait()
-
     def rows_of(y2):
         return pl.ds(pl.multiple_of(y2 * ROWS_EACH, ROWS_EACH), ROWS_EACH)
 
-    own_rows = rows_of(dp)
-    ring = {"x": [(1, 0, 0), (3, 0, 0), (2, 0, 0)], "y": [(0, 1, 0), (0, 3, 0), (0, 2, 0)]}
-    first_peers = {
-        "x": [(2, 0, 0), (1, 0, 0), (3, 0, 0)],
-        "y": [(0, 2, 0), (0, 1, 0), (0, 3, 0)],
-        "z": [(0, 0, 1)],
-    }
     second_peers = {
         "x": [(0, dy, dz) for dy in (2, 1, 3, 0) for dz in (1, 0) if dy or dz],
         "y": [(dx, 0, dz) for dx in (2, 1, 3, 0) for dz in (1, 0) if dx or dz],
@@ -283,130 +313,70 @@
     def wait_send(i, like):
         remote(like, like, i, peer(FAR_FIRST[-1])[1]).wait_send()
 
-    base = 7
-    step_a, step_b, step_c, step_2, step_3, step_4 = (base + 5 * i for i in range(6))
-    for p, (kind, first, count) in enumerate(CHUNKS):
-        out, arrived = gu_out[p], gu_in1[p]
-        width = count * 128
-        for c in range(SECTIONS):
+    step_0, step_1, step_2, step_3, step_4 = (7 + N_CHUNKS * i for i in range(5))
+    for p, (kind, _, _) in enumerate(CHUNKS):
+        wide_rows[p][:, 0:COLS] = scaled
+        for offset in ring[kind]:
+            to = wide_rows[p].at[:, pl.ds(step_of(offset) * COLS, COLS)]
+            send(step_1 + p, wide_rows[p].at[:, pl.ds(0, COLS)], to, at(*offset)[3])
+    for offset in FAR_FIRST:
+        remote(sq_out, sq_in.at[rank], 3, peer(offset)[1]).start()
+    row_place = {"x": dp, "y": x, "z": dp}
+    for p, (kind, _, count) in enumerate(CHUNKS):
+        whole = wide_weights[p].at[:, :, pl.ds(0, 128)]
+        pltpu.make_async_copy(whole, whole, own_rows_sem.at[p]).wait()
+        wait_recv(step_0 + p, wide_weights[p].at[:, :, pl.ds(128, 128 * (WAYS[kind] - 1))])
+        wait_recv(step_1 + p, wide_rows[p].at[:, pl.ds(COLS, COLS * (WAYS[kind] - 1))])
+        for i in range(NX if kind == "z" else NZ):
             for half in range(2):
-                start = c * UNITS_EACH + first * 128
-                product = jnp.dot(
-                    scaled, gate_up[half, :, start : start + width], preferred_element_type=F32
+                gu_sum[p][i, half] = jnp.dot(
+                    wide_rows[p][...], wide_weights[p][i, half], preferred_element_type=F32
                 ).astype(BF16)
-                if kind == "x":
-                    out[c // NZ, c % NZ, half] = product
-                elif kind == "y":
-                    for y2 in range(NY):
-                        out[y2, c // 4, c % 4, half] = product[y2 * ROWS_EACH : (y2 + 1) * ROWS_EACH]
-                else:
-                    out[c % NZ, c // NZ, half] = product
-        if kind == "z":
-            _, _, z2, device = at(0, 0, 1)
-            send(step_a + p, out.at[z2], arrived.at[0], device)
-            continue
-        along = 0 if kind == "x" else 1
-        after, before, across = ring[kind]
-        far, right, left = at(*across)[along], at(*after), at(*before)
-        send(step_a + p, out.at[far, 0], arrived.at[0, 0], right[3])
-        send(step_a + p, out.at[far, 1], arrived.at[0, 1], left[3])
-        send(step_b + p, out.at[right[along], 1], arrived.at[1, 1], right[3])
-        send(step_b + p, out.at[left[along], 0], arrived.at[1, 0], left[3])
-    for p, (kind, first, count) in enumerate(CHUNKS):
-        if kind == "z":
-            continue
-        out, arrived = gu_out[p], gu_in1[p]
-        along = 0 if kind == "x" else 1
-        after, before, _ = ring[kind]
-        right, left = at(*after), at(*before)
-        wait_recv(step_a + p, arrived.at[0])
-        passed = gu_passed[p]
-        for i, (to, device) in enumerate(((right[along], right[3]), (left[along], left[3]))):
-
-            def merge(j, carry):
-                passed[i, j] = (out[to, i, j].astype(F32) + arrived[0, i, j].astype(F32)).astype(BF16)
-                return carry
-
-            lax.fori_loop(0, passed.shape[1], merge, 0, unroll=True)
-            send(step_c + p, passed.at[i], arrived.at[2, i], device)
-    for p, (kind, first, count) in enumerate(CHUNKS):
-        out, arrived, total, arrived2 = gu_out[p], gu_in1[p], gu_sum[p], gu_in2[p]
-        if kind == "z":
-            wait_recv(step_a + p, arrived)
-
-            def add(i, carry):
-                total[i] = (out[z, i].astype(F32) + arrived[0, i].astype(F32)).astype(BF16)
-                return carry
-
-            lax.fori_loop(0, total.shape[0], add, 0)
-        else:
-            wait_recv(step_b + p, arrived.at[1])
-            wait_recv(step_c + p, arrived.at[2])
-            mine = x if kind == "x" else dp
-            for i in range(2):
-
-                def add(j, carry):
-                    value = out[mine, i, j].astype(F32) + arrived[1, i, j].astype(F32)
-                    total[i, j] = (value + arrived[2, i, j].astype(F32)).astype(BF16)
-                    return carry
-
-                lax.fori_loop(0, total.shape[1], add, 0, unroll=True)
         for k, offset in enumerate(second_peers[kind]):
             x2, y2, z2, device = at(*offset)
-            if kind == "x":
-                src = total.at[z2, :, rows_of(y2)]
-            elif kind == "y":
-                src = total.at[x2 // 2, lax.rem(x2, 2) * NZ + z2]
-            else:
-                src = total.at[x2, :, rows_of(y2)]
-            send(step_2 + p, src, arrived2.at[k], device)
+            src = gu_sum[p].at[x2 if kind == "z" else z2, :, rows_of({"x": y2, "y": x2, "z": y2}[kind])]
+            send(step_2 + p, src, gu_in2[p].at[k], device)
 
     wait_all(sq_in.at[rest], sq_in.at[rest], 3)
     total = jnp.sum(sq_in[...], axis=0)
-    row_of = lax.broadcasted_iota(jnp.int32, (ROWS_EACH, HD), 0) + dp * ROWS_EACH
     lane_of = lax.broadcasted_iota(jnp.int32, (ROWS_EACH, HD), 1)
-    total = jnp.sum(jnp.where(row_of == lane_of, total, 0.0), axis=1, keepdims=True)
-    factor = lax.rsqrt(total / D + 1e-05)
+    factors = {}
+    for kind in "xy":
+        row_of = lax.broadcasted_iota(jnp.int32, (ROWS_EACH, HD), 0) + row_place[kind] * ROWS_EACH
+        square = jnp.sum(jnp.where(row_of == lane_of, total, 0.0), axis=1, keepdims=True)
+        factors[kind] = lax.rsqrt(square / D + 1e-05)
+    factors["z"] = factors["x"]
 
     def like_3(p):
         return gu_in2[p].at[:, 0]
 
     def like_4(p):
-        return gu_in1[p].at[0, :, 0] if CHUNKS[p][0] == "z" else gu_in1[p].at[:, 0]
+        if CHUNKS[p][0] == "z":
+            return gu_sum[p].at[:, 0]
+        return act[p].at[pl.ds(0, 3)]
 
     def activate(p):
         kind = CHUNKS[p][0]
-        total, arrived2, part = gu_sum[p], gu_in2[p], act[p]
-        wait_recv(step_2 + p, arrived2)
+        wait_recv(step_2 + p, gu_in2[p])
+        mine = rows_of(row_place[kind])
         halves = []
         for half in range(2):
-            if kind == "x":
-                value = total[z, half, own_rows]
-            elif kind == "y":
-                value = total[x // 2, lax.rem(x, 2) * NZ + z, half]
-            else:
-                value = total[x, half, own_rows]
-            value = value.astype(F32)
+            value = gu_sum[p][x if kind == "z" else z, half, mine].astype(F32)
             for k in range(len(second_peers[kind])):
-                value = value + arrived2[k, half].astype(F32)
-            halves.append(value * factor)
+                value = value + gu_in2[p][k, half].astype(F32)
+            halves.append(value * factors[kind])
         gate, up = halves
-        part[x, z, own_rows] = (gate / (1.0 + jnp.exp(-gate)) * up).astype(BF16)
-        block = part.at[x, z, own_rows]
+        major = dp if kind == "y" else x
+        act[p][major, z, mine] = (gate / (1.0 + jnp.exp(-gate)) * up).astype(BF16)
+        block = act[p].at[major, z, mine]
         for offset in second_peers[kind]:
             send(step_3 + p, block, block, at(*offset)[3])
 
     def pass_on(p):
         kind = CHUNKS[p][0]
-        part = act[p]
         wait_recv(step_3 + p, like_3(p))
-        if kind == "x":
-            block = part.at[x]
-        elif kind == "y":
-            block = part.at[:, :, own_rows]
-        else:
-            block = part.at[:, z]
-        for offset in first_peers[kind]:
+        block = {"x": act[p].at[x], "y": act[p].at[dp], "z": act[p].at[:, z]}[kind]
+        for offset in ring[kind]:
             send(step_4 + p, block, block, at(*offset)[3])
 
     def lower(p):
@@ -422,21 +392,18 @@
             partial = product if partial is None else partial + product
         lowered_sum[...] = partial if p == 0 else lowered_sum[...] + partial
 
-    for p in range(5):
+    for p in range(N_CHUNKS):
         activate(p)
-    for p in range(5):
+    for p in range(N_CHUNKS):
         pass_on(p)
     loads[8].wait()
-    for p in range(5):
+    for p in range(N_CHUNKS):
         lower(p)
     partial = lowered_sum[...]
     lowered = sum_over_tensor(partial, proj2, 6)
-    for p in range(5):
-        if CHUNKS[p][0] == "z":
-            wait_send(step_a + p, gu_in1[p])
-        else:
-            for i, step in enumerate((step_a, step_b, step_c)):
-                wait_send(step + p, gu_in1[p].at[i])
+    for p, (kind, _, _) in enumerate(CHUNKS):
+        wait_send(step_0 + p, wide_weights[p].at[:, :, pl.ds(128, 128 * (WAYS[kind] - 1))])
+        wait_send(step_1 + p, wide_rows[p].at[:, pl.ds(COLS, COLS * (WAYS[kind] - 1))])
         wait_send(step_2 + p, gu_in2[p])
         wait_send(step_3 + p, like_3(p))
         wait_send(step_4 + p, like_4(p))
@@ -444,22 +411,17 @@
 
 
 def chunk_buffers():
-    out, in1, passed, total, in2, act = [], [], [], [], [], []
+    weights, rows, total, in2, act = [], [], [], [], []
     for kind, first, count in CHUNKS:
         w = count * 128
-        if kind == "z":
-            shape, arrived, peers = (NX, 2, B, w), (1, NX, 2, B, w), NX * NY - 1
-            kept = (8, w)
-        else:
-            shape = {"x": (2, 2, B, w), "y": (2, 4, 2, ROWS_EACH, w)}[kind]
-            arrived, kept, peers = (3, *shape), shape, 7
-        out.append(pltpu.VMEM(({"x": NX, "y": NY, "z": NZ}[kind], *shape), BF16))
-        in1.append(pltpu.VMEM(arrived, BF16))
-        passed.append(pltpu.VMEM(kept, BF16))
-        total.append(pltpu.VMEM(shape, BF16))
+        blocks, peers = (NX, NX * NY - 1) if kind == "z" else (NZ, NX * NZ - 1)
+        weights.append(pltpu.VMEM((blocks, 2, COLS * WAYS[kind], w), BF16))
+        rows.append(pltpu.VMEM((B, COLS * WAYS[kind]), BF16))
+        total.append(pltpu.VMEM((blocks, 2, B, w), BF16))
         in2.append(pltpu.VMEM((peers, 2, ROWS_EACH, w), BF16))
         act.append(pltpu.VMEM((NX, NZ, B, w), BF16))
-    return [*out, *in1, *passed, *total, *in2, *act, pltpu.VMEM((B, COLS), F32)]
+    sums = [pltpu.VMEM((B, COLS), F32), pltpu.SemaphoreType.DMA((N_CHUNKS,))]
+    return [*weights, *rows, *total, *in2, *act, *sums]
 
 
 def body(
@@ -494,7 +456,6 @@
             pltpu.VMEM(cache_keys.shape, BF16),
             pltpu.VMEM(cache_values.shape, BF16),
             pltpu.VMEM(out_weight.shape, BF16),
-            pltpu.VMEM(gate_up.shape, BF16),
             pltpu.VMEM(down_weight.shape, BF16),
             pltpu.VMEM((B * SLOT_ROWS, HD), F32),
             pltpu.VMEM((RANKS, SEQS * SLOT_ROWS, HD), BF16),
@@ -508,8 +469,8 @@
             pltpu.VMEM((RANKS, 1, 128), F32),
             *chunk_buffers(),
             pltpu.SemaphoreType.DMA((12,)),
-            pltpu.SemaphoreType.DMA((37,)),
-            pltpu.SemaphoreType.DMA((37,)),
+            pltpu.SemaphoreType.DMA((7 + 5 * N_CHUNKS,)),
+            pltpu.SemaphoreType.DMA((7 + 5 * N_CHUNKS,)),
         ],
         compiler_params=pltpu.CompilerParams(
             collective_id=0, has_side_effects=True, vmem_limit_bytes=32 * 2**20

time: 60.4 us -> 57.9 us (0.959)
  Pallas kernels: 59.6 us -> 57.2 us
    pallas_call x1, Pallas kernels: 59.6 us -> 57.2 us  [body(): pl.pallas_call(layer_kernel, out_shape=jax.ShapeDtypeStruct((B, COLS), F3...]
where the time goes in v4:
time: 57.9 us; the launch traced here: 57.8 us
  Pallas kernels  57.2 us (99%)
  other arithmetic  0.61 us (1%)
    pallas_call x1, Pallas kernels, body(): pl.pallas_call(layer_kernel, out_shape=jax.ShapeDtypeStruct((B, COLS), F3...  57.2 us

profile of v4, /device:TPU:1, one launch (start us, length us, event | category | flops | bytes accessed | tf_op | source)
XLA Modules:
  0.0 57.8 jit_solution(11657336882076399979)
XLA Ops:
  0.0 57.2 %decoder_layer.1 = f32[64,128]{1,0:T(8,128)S(1)} custom-call(s32[10]{0:T(128)} %order_hbm.1, s32[2]{0:T(128)} %len_hbm.1, f32[1,128]{1,0:T(1,128)} %constant.2.clone.freq_hbm, bf16[64,128]{1,0:T(8,128)(2,1)} %tokens_hbm.1, f32[1,128]{1,0:T(1,128)} %bitcast.2, f32[1,128]{1,0:T(1,128)} %bitcast.3, bf16[128,2560]{1,0:T(8,128)(2,1)} %qkv_hbm.1, ...), custom_call_target="tpu_custom_call" | custom-call | tf_op jit(solution)/shard_map/decoder_layer/pallas_call | solution.py:444
  57.2 0.6 %convert_element_type.3 = bf16[64,128]{1,0:T(8,128)(2,1)} convert(f32[64,128]{1,0:T(8,128)S(1)} %decoder_layer.1) | non-fusion elementwise | flops 8192 | bytes 49152 | tf_op jit(solution)/shard_map/convert_element_type | solution.py:498

commit v5 on v4

--- a/solution.py
+++ b/solution.py
@@ -32,10 +32,11 @@
     [(dx, dy, dz) for dx in range(NX) for dy in range(NY) for dz in range(NZ) if dx or dy or dz],
     key=lambda o: -(min(o[0], NX - o[0]) + min(o[1], NY - o[1]) + 2 * o[2]),
 )
-CHUNKS = (("x", 0, 3), ("y", 3, 2), ("z", 5, 2))
+CHUNKS = (("x", 0, 2), ("y", 2, 2), ("z", 4, 2))
+LAST = 6
 N_CHUNKS = len(CHUNKS)
 WAYS = {"x": NX, "y": NY, "z": NZ}
-BATCHES = {"x": (6, 4, 2), "y": (6, 4, 2), "z": (4, 2, 2)}
+BATCHES = {"x": (4, 8, 0), "y": (4, 8, 0), "z": (3, 5, 0)}
 MESH = pl.DeviceIdType.MESH
 F32 = jnp.float32
 BF16 = jnp.bfloat16
@@ -78,7 +79,8 @@
     *rest_refs,
 ):
     wide_weights, wide_rows, gu_sum, gu_in2, act = (rest_refs[N_CHUNKS * i : N_CHUNKS * (i + 1)] for i in range(5))
-    lowered_sum, own_rows_sem, load_sem, send_sem, recv_sem = rest_refs[5 * N_CHUNKS :]
+    last_weights, last_sum, last_in, last_act = rest_refs[5 * N_CHUNKS : 5 * N_CHUNKS + 4]
+    lowered_sum, own_rows_sem, load_sem, send_sem, recv_sem = rest_refs[5 * N_CHUNKS + 4 :]
     section = lax.axis_index("section")
     x = section // NZ
     z = lax.rem(section, NZ)
@@ -196,6 +198,10 @@
                 pltpu.make_async_copy(
                     weight_piece(p, place[kind], i, half), wide_weights[p].at[i, half, pl.ds(0, 128)], own_rows_sem.at[p]
                 ).start()
+
+    for c in range(SECTIONS):
+        src = gate_up_hbm.at[:, :, pl.ds(c * UNITS_EACH + LAST * 128, 128)]
+        pltpu.make_async_copy(src, last_weights.at[c], own_rows_sem.at[N_CHUNKS]).start()
 
     def send_weights(batch):
         for p, (kind, _, _) in enumerate(CHUNKS):
@@ -319,6 +325,14 @@
         for offset in ring[kind]:
             to = wide_rows[p].at[:, pl.ds(step_of(offset) * COLS, COLS)]
             send(step_1 + p, wide_rows[p].at[:, pl.ds(0, COLS)], to, at(*offset)[3])
+    pltpu.make_async_copy(last_weights, last_weights, own_rows_sem.at[N_CHUNKS]).wait()
+    for c in range(SECTIONS):
+        for half in range(2):
+            product = jnp.dot(scaled, last_weights[c, half], preferred_element_type=F32)
+            last_sum[c, half] = product.astype(BF16)
+    for k, offset in enumerate(FAR_FIRST):
+        x2, y2, z2, device = at(*offset)
+        send(4, last_sum.at[x2 * NZ + z2, :, rows_of(y2)], last_in.at[k], device)
     for offset in FAR_FIRST:
         remote(sq_out, sq_in.at[rank], 3, peer(offset)[1]).start()
     row_place = {"x": dp, "y": x, "z": dp}
@@ -347,6 +361,31 @@
         factors[kind] = lax.rsqrt(square / D + 1e-05)
     factors["z"] = factors["x"]
 
+    def activate_last():
+        wait_recv(4, last_in)
+        mine = rows_of(dp)
+        halves = []
+        for half in range(2):
+            value = last_sum[section, half, mine].astype(F32)
+            for k in range(RANKS - 1):
+                value = value + last_in[k, half].astype(F32)
+            halves.append(value * factors["x"])
+        gate, up = halves
+        last_act[section, mine] = (gate / (1.0 + jnp.exp(-gate)) * up).astype(BF16)
+        block = last_act.at[section, mine]
+        for offset in FAR_FIRST:
+            send(5, block, block, at(*offset)[3])
+
+    def lower_last():
+        wait_recv(5, last_in.at[:, 0])
+        partial = jnp.zeros((B, COLS), F32)
+        for c in range(SECTIONS):
+            start = c * UNITS_EACH + LAST * 128
+            partial = partial + jnp.dot(
+                last_act[c], down[start : start + 128], preferred_element_type=F32
+            )
+        lowered_sum[...] = partial
+
     def like_3(p):
         return gu_in2[p].at[:, 0]
 
@@ -390,17 +429,21 @@
                 act[p][c // NZ, c % NZ], down[start : start + width], preferred_element_type=F32
             )
             partial = product if partial is None else partial + product
-        lowered_sum[...] = partial if p == 0 else lowered_sum[...] + partial
+        lowered_sum[...] = lowered_sum[...] + partial
 
     for p in range(N_CHUNKS):
         activate(p)
+    activate_last()
     for p in range(N_CHUNKS):
         pass_on(p)
     loads[8].wait()
+    lower_last()
     for p in range(N_CHUNKS):
         lower(p)
     partial = lowered_sum[...]
     lowered = sum_over_tensor(partial, proj2, 6)
+    wait_send(4, last_in)
+    wait_send(5, last_in.at[:, 0])
     for p, (kind, _, _) in enumerate(CHUNKS):
         wait_send(step_0 + p, wide_weights[p].at[:, :, pl.ds(128, 128 * (WAYS[kind] - 1))])
         wait_send(step_1 + p, wide_rows[p].at[:, pl.ds(COLS, COLS * (WAYS[kind] - 1))])
@@ -420,7 +463,14 @@
         total.append(pltpu.VMEM((blocks, 2, B, w), BF16))
         in2.append(pltpu.VMEM((peers, 2, ROWS_EACH, w), BF16))
         act.append(pltpu.VMEM((NX, NZ, B, w), BF16))
-    sums = [pltpu.VMEM((B, COLS), F32), pltpu.SemaphoreType.DMA((N_CHUNKS,))]
+    sums = [
+        pltpu.VMEM((SECTIONS, 2, COLS, 128), BF16),
+        pltpu.VMEM((SECTIONS, 2, B, 128), BF16),
+        pltpu.VMEM((RANKS - 1, 2, ROWS_EACH, 128), BF16),
+        pltpu.VMEM((SECTIONS, B, 128), BF16),
+        pltpu.VMEM((B, COLS), F32),
+        pltpu.SemaphoreType.DMA((N_CHUNKS + 1,)),
+    ]
     return [*weights, *rows, *total, *in2, *act, *sums]
 
 

time: 57.9 us -> 55.2 us (0.953)
  Pallas kernels: 57.2 us -> 54.4 us
    pallas_call x1, Pallas kernels: 57.2 us -> 54.4 us  [body(): pl.pallas_call(layer_kernel, out_shape=jax.ShapeDtypeStruct((B, COLS), F3...]
where the time goes in v5:
time: 55.2 us; the launch traced here: 55 us
  Pallas kernels  54.4 us (99%)
  other arithmetic  0.61 us (1%)
    pallas_call x1, Pallas kernels, body(): pl.pallas_call(layer_kernel, out_shape=jax.ShapeDtypeStruct((B, COLS), F3...  54.4 us

profile of v5, /device:TPU:1, one launch (start us, length us, event | category | flops | bytes accessed | tf_op | source)
XLA Modules:
  0.0 55.0 jit_solution(7478328205387850916)
XLA Ops:
  0.0 54.4 %decoder_layer.1 = f32[64,128]{1,0:T(8,128)S(1)} custom-call(s32[10]{0:T(128)} %order_hbm.1, s32[2]{0:T(128)} %len_hbm.1, f32[1,128]{1,0:T(1,128)} %constant.2.clone.freq_hbm, bf16[64,128]{1,0:T(8,128)(2,1)} %tokens_hbm.1, f32[1,128]{1,0:T(1,128)} %bitcast.2, f32[1,128]{1,0:T(1,128)} %bitcast.3, bf16[128,2560]{1,0:T(8,128)(2,1)} %qkv_hbm.1, ...), custom_call_target="tpu_custom_call" | custom-call | tf_op jit(solution)/shard_map/decoder_layer/pallas_call | solution.py:494
  54.4 0.6 %convert_element_type.3 = bf16[64,128]{1,0:T(8,128)(2,1)} convert(f32[64,128]{1,0:T(8,128)S(1)} %decoder_layer.1) | non-fusion elementwise | flops 8192 | bytes 49152 | tf_op jit(solution)/shard_map/convert_element_type | solution.py:548

commit v6 on v5

--- a/solution.py
+++ b/solution.py
@@ -36,7 +36,7 @@
 LAST = 6
 N_CHUNKS = len(CHUNKS)
 WAYS = {"x": NX, "y": NY, "z": NZ}
-BATCHES = {"x": (4, 8, 0), "y": (4, 8, 0), "z": (3, 5, 0)}
+BATCHES = {"x": (4,7,1), "y": (4,7,1), "z": (4,4,0)}
 MESH = pl.DeviceIdType.MESH
 F32 = jnp.float32
 BF16 = jnp.bfloat16
@@ -272,7 +272,7 @@
         att32[pl.ds(i * SEQS * LOCAL_HEADS, SEQS * LOCAL_HEADS)] = att_in[i].astype(F32)
         return carry
 
-    lax.fori_loop(0, RANKS, widen, 0)
+    lax.fori_loop(0, RANKS, widen, 0, unroll=True)
     loads[6].wait()
     attended = jnp.concatenate([att32[pl.Slice(h, B, LOCAL_HEADS)].astype(BF16) for h in range(LOCAL_HEADS)], axis=1)
     partial = jnp.dot(attended, outw[...], preferred_element_type=F32)

time: 55.2 us -> 54.9 us (level)
  no operation moved by 1% of the time
where the time goes in v6:
time: 54.9 us; the launch traced here: 54.8 us
  Pallas kernels  54.1 us (99%)
  other arithmetic  0.61 us (1%)
    pallas_call x1, Pallas kernels, body(): pl.pallas_call(layer_kernel, out_shape=jax.ShapeDtypeStruct((B, COLS), F3...  54.1 us

profile of v6, /device:TPU:1, one launch (start us, length us, event | category | flops | bytes accessed | tf_op | source)
XLA Modules:
  0.0 54.8 jit_solution(14042711352301267236)
XLA Ops:
  0.0 54.1 %decoder_layer.1 = f32[64,128]{1,0:T(8,128)S(1)} custom-call(s32[10]{0:T(128)} %order_hbm.1, s32[2]{0:T(128)} %len_hbm.1, f32[1,128]{1,0:T(1,128)} %constant.2.clone.freq_hbm, bf16[64,128]{1,0:T(8,128)(2,1)} %tokens_hbm.1, f32[1,128]{1,0:T(1,128)} %bitcast.2, f32[1,128]{1,0:T(1,128)} %bitcast.3, bf16[128,2560]{1,0:T(8,128)(2,1)} %qkv_hbm.1, ...), custom_call_target="tpu_custom_call" | custom-call | tf_op jit(solution)/shard_map/decoder_layer/pallas_call | solution.py:494
  54.2 0.6 %convert_element_type.3 = bf16[64,128]{1,0:T(8,128)(2,1)} convert(f32[64,128]{1,0:T(8,128)S(1)} %decoder_layer.1) | non-fusion elementwise | flops 8192 | bytes 49152 | tf_op jit(solution)/shard_map/convert_element_type | solution.py:548
